TPU v7x, 64 devices: a 2x2x8 block of a 4x4x8 slice. The times are simulated.
64 devices in a mesh: rep: 4 (over x, y), dp: 16 (over z, core).
Axes of the slice: x: 2, y: 2, z: 8, core: 2. Of those that a mesh axis runs over, the one named last changes fastest.
The devices are a block of a 4x4x8 slice.
Arguments:
- x: bfloat16 [64, 2048, 768], P(('rep', 'dp')), parts along dimension 0
- dy: bfloat16 [64, 2048, 768], P(('rep', 'dp')), parts along dimension 0
- w_gate: bfloat16 [2, 768, 2304], replicated
- w_up: bfloat16 [2, 768, 2304], replicated
- w_down: bfloat16 [2, 2304, 768], replicated
- m_w_gate: float32 [2, 768, 2304], P(None, 'dp')
- m_w_up: float32 [2, 768, 2304], P(None, 'dp')
- m_w_down: float32 [2, 2304, 768], P(None, 'dp')
- v_w_gate: float32 [2, 768, 2304], P(None, 'dp')
- v_w_up: float32 [2, 768, 2304], P(None, 'dp')
- v_w_down: float32 [2, 2304, 768], P(None, 'dp')
Outputs:
- output 1: bfloat16 [8, 768, 2304], P('rep'), parts along dimension 0
- output 2: bfloat16 [8, 768, 2304], P('rep'), parts along dimension 0
- output 3: bfloat16 [8, 2304, 768], P('rep'), parts along dimension 0
- output 4: float32 [8, 768, 2304], P('rep', 'dp'), parts along dimension 0
- output 5: float32 [8, 768, 2304], P('rep', 'dp'), parts along dimension 0
- output 6: float32 [8, 2304, 768], P('rep', 'dp'), parts along dimension 0
- output 7: float32 [8, 768, 2304], P('rep', 'dp'), parts along dimension 0
- output 8: float32 [8, 768, 2304], P('rep', 'dp'), parts along dimension 0
- output 9: float32 [8, 2304, 768], P('rep', 'dp'), parts along dimension 0
There are 4 independent parts. A program takes and returns all parts, laid end to end along the dimension named above; an argument that names none is the same for every part.
All inputs are finite; a program needn't handle non-finite values.
Results may differ from a plain program's by a relative error of at most 0.022.
Values are sent between devices in bfloat16 or wider.
A program may use at most 768 MiB of HBM per device.

v0:
```python
import jax
import jax.numpy as jnp
from jax import lax

NAMES = ("w_gate", "w_up", "w_down")


def matmul(a, w):
    return jnp.dot(a, w, preferred_element_type=jnp.float32).astype(jnp.bfloat16)


def normed(h):
    wide = h.astype(jnp.float32)
    scale = lax.rsqrt(jnp.mean(wide**2, -1, keepdims=True) + 1e-6)
    return (wide * scale).astype(jnp.bfloat16)


def layer(h, w):
    a = normed(h)
    gate = jnp.dot(a, w["w_gate"], preferred_element_type=jnp.float32)
    up = jnp.dot(a, w["w_up"], preferred_element_type=jnp.float32)
    return h + matmul((jax.nn.silu(gate) * up).astype(jnp.bfloat16), w["w_down"])


def adamw(w, m, v, g):
    m = 0.9 * m + 0.1 * g
    v = 0.95 * v + 0.05 * g * g
    step = m * lax.rsqrt(v + 1e-8) + 0.1 * w
    return (w - 0.02 * step).astype(jnp.bfloat16), m, v


def stack(weights, h):
    for number in range(weights["w_gate"].shape[0]):
        h = layer(h, {name: w[number] for name, w in weights.items()})
    return h


def solution(mesh):
    groups = mesh.shape["rep"]

    def step(x, dy, *arrays):
        weights, m, v = (arrays[i : i + 3] for i in (0, 3, 6))
        x, dy = (t.reshape(groups, -1, *t.shape[1:]) for t in (x, dy))

        def of_a_group(x, dy):
            _, back = jax.vjp(lambda w: stack(w, x), dict(zip(NAMES, weights, strict=True)))
            by_weights = back(dy)[0]
            gradients = [by_weights[name].astype(jnp.float32) for name in NAMES]
            new = [adamw(w.astype(jnp.float32), m, v, g) for w, m, v, g in zip(weights, m, v, gradients, strict=True)]
            return tuple(one[which] for which in range(3) for one in new)

        return tuple(t.reshape(-1, *t.shape[2:]) for t in jax.vmap(of_a_group)(x, dy))

    return step
```

profile of v0, /device:TPU:21, one launch (start us, length us, event | category | flops | bytes accessed | tf_op | source)
XLA Modules:
  0.0 974.2 jit_solution(1466078520931365061)
XLA Ops:
  17.5 12.5 %fusion.160 = bf16[1,1,2048,2304]{3,2,1,0:T(8,128)(2,1)} fusion(bf16[2,2304,768]{2,1,0:T(8,128)(2,1)} %param.16, bf16[1,2048,768]{2,1,0:T(8,128)(2,1)} %param.17), kind=kOutput, calls=%fused_computation.204 | convolution fusion | flops 7252475904 | bytes 16121856 | tf_op jit(solution)/vmap(transpose(jvp()))/dot_general | solution.py:9
  30.0 12.9 %fusion.182 = f32[2048,2304]{1,0:T(8,128)} fusion(bf16[2,768,2304]{2,1,0:T(8,128)(2,1)} %param.12, bf16[1,2048,768]{2,1,0:T(8,128)(2,1)S(1)} %copy-done.6, f32[2048]{0:T(1024)S(1)} %add_rsqrt_fusion), kind=kOutput, calls=%fused_computation.230 | convolution fusion | flops 7252475904 | bytes 25567232 | tf_op jit(solution)/vmap(jvp())/dot_general | solution.py:20
  42.9 20.4 %fusion.156 = (bf16[1,1,2048,2304]{3,2,1,0:T(8,128)(2,1)}, f32[2048,2304]{1,0:T(8,128)}) fusion(f32[2048,2304]{1,0:T(8,128)} %fusion.182, bf16[2,768,2304]{2,1,0:T(8,128)(2,1)} %param.15, bf16[1,2048,768]{2,1,0:T(8,128)(2,1)S(1)} %copy-done.6, f32[2048]{0:T(1024)S(1)} %add_rsqrt_fusion), kind=kOutput, calls=%fused_computation.191 | convolution fusion | flops 7280787456 | bytes 53878784 | tf_op jit(solution)/vmap(jvp())/dot_general | solution.py:21
  63.4 12.9 %fusion.168 = (f32[2048]{0:T(1024)S(1)}, bf16[1,1,2048,768]{2,3,1,0:T(8,128)(2,1)S(1)}) fusion(bf16[2,2304,768]{2,1,0:T(8,128)(2,1)} %param.16, bf16[1,1,2048,2304]{3,2,1,0:T(8,128)(2,1)} %get-tuple-element.263, bf16[1,2048,768]{1,2,0:T(8,128)(2,1)} %copy), kind=kOutput, calls=%fused_computation.215 | convolution fusion | flops 7255619584 | bytes 19275776 | tf_op jit(solution)/vmap(jvp())/dot_general | solution.py:9
  78.8 10.8 %fusion.175 = f32[2048,2304]{1,0:T(8,128)} fusion(bf16[1,1,2048,768]{2,3,1,0:T(8,128)(2,1)S(1)} %fusion.169, bf16[2,768,2304]{2,1,0:T(8,128)(2,1)S(1)} %bitcast.654), kind=kOutput, calls=%fused_computation.223 | convolution fusion | flops 7247757312 | bytes 25559040 | tf_op jit(solution)/vmap(jvp())/dot_general | solution.py:21
  89.7 27.8 %fusion.145 = (bf16[1,1,2048,2304]{3,2,1,0:T(8,128)(2,1)}, bf16[1,1,2048,2304]{3,2,1,0:T(8,128)(2,1)}, f32[2048,2304]{1,0:T(8,128)}) fusion(f32[2048,2304]{1,0:T(8,128)} %fusion.175, bf16[1,1,2048,2304]{3,2,1,0:T(8,128)(2,1)} %fusion.160, bf16[2,768,2304]{2,1,0:T(8,128)(2,1)} %param.12, bf16[1,1,2048,768]{2,3,1,0:T(8,128)(2,1)S(1)} %fusion.169), kind=kOutput, calls=%fused_computation.175 | convolution fusion | flops 7318536192 | bytes 72744960 | tf_op jit(solution)/vmap(jvp())/dot_general | solution.py:20
  117.4 17.4 %fusion.155 = bf16[1,1,2048,2304]{3,2,1,0:T(8,128)(2,1)} fusion(f32[2048,2304]{1,0:T(8,128)} %fusion.175, f32[2048,2304]{1,0:T(8,128)} %get-tuple-element.267), kind=kLoop, calls=%fused_computation.189 | loop fusion | flops 28311552 | bytes 47185920 | tf_op jit(solution)/vmap(jvp())/convert_element_type | solution.py:22
  134.9 12.7 %copy.2 = bf16[1,1,2048,2304]{2,3,1,0:T(8,128)(2,1)} copy(bf16[1,1,2048,2304]{3,2,1,0:T(8,128)(2,1)} %fusion.155) | data formatting | bytes 18874368
  150.8 104.1 %while.16 = (bf16[1,1,2048,2304]{2,3,1,0:T(8,128)(2,1)}, bf16[1,1,2048,768]{3,2,1,0:T(8,128)(2,1)S(1)}, f32[1,144,768]{2,1,0:T(8,128)}, f32[1,144,768]{2,1,0:T(8...) while((bf16[1,1,2048,2304]{2,3,1,0:T(8,128)(2,1)}, ...), condition=%wide.windowed_dot_general_cond_rs.4.clone, body=%wide.windowed_dot_general_body_rs.4.clone.sunk | while | flops 1817321472 | bytes 41091684 | solution.py:9
  254.8 12.7 %copy.4 = bf16[1,1,2048,2304]{2,3,1,0:T(8,128)(2,1)} copy(bf16[1,1,2048,2304]{3,2,1,0:T(8,128)(2,1)} %get-tuple-element.263) | data formatting | bytes 18874368
  267.5 11.3 %fusion.192 = bf16[2048,768]{0,1:T(8,128)(2,1)S(1)} fusion(bf16[1,1,2048,2304]{3,2,1,0:T(8,128)(2,1)} %get-tuple-element.622, bf16[2,768,2304]{2,1,0:T(8,128)(2,1)} %param.15), kind=kOutput, calls=%fused_computation.236 | convolution fusion | flops 7247757312 | bytes 16121856 | tf_op jit(solution)/vmap(transpose(jvp()))/dot_general | solution.py:21
  278.9 11.6 %fusion.170 = (f32[2048]{0:T(1024)S(1)}, bf16[2048,768]{0,1:T(8,128)(2,1)S(1)}) fusion(bf16[1,1,2048,768]{2,3,1,0:T(8,128)(2,1)S(1)} %copy-done.8, bf16[2048,768]{0,1:T(8,128)(2,1)S(1)} %fusion.192, bf16[2,768,2304]{2,1,0:T(8,128)(2,1)} %param.12, bf16[1,1,2048,2304]{3,2,1,0:T(8,128)(2,1)} %get-tuple-element.544), kind=kOutput, calls=%fused_computation.217 | convolution fusion | flops 7255619584 | bytes 22421504 | tf_op jit(solution)/vmap(transpose(jvp()))/dot_general | solution.py:20
  299.0 101.6 %while.17 = (bf16[1,1,2048,2304]{2,3,1,0:T(8,128)(2,1)}, bf16[1,1,2048,768]{3,2,1,0:T(8,128)(2,1)}, f32[1,144,768]{2,1,0:T(8,128)}, f32[1,144,768]{2,1,0:T(8,128...) while((bf16[1,1,2048,2304]{2,3,1,0:T(8,128)(2,1)}, ...), condition=%wide.windowed_dot_general_cond_rs.5.clone, body=%wide.windowed_dot_general_body_rs.5.clone.sunk | while | flops 1817321472 | bytes 41091684 | solution.py:9
  400.6 101.4 %while.14 = (bf16[1,1,2048,768]{2,3,1,0:T(8,128)(2,1)S(1)}, bf16[1,1,2048,2304]{3,2,1,0:T(8,128)(2,1)}, f32[1,48,2304]{2,1,0:T(8,128)}, f32[1,48,2304]{2,1,0:T(8...) while((bf16[1,1,2048,768]{2,3,1,0:T(8,128)(2,1)S(1)}, ...), condition=%wide.windowed_dot_general_cond_rs.2.clone, body=%wide.windowed_dot_general_body_rs.2.clone.sunk | while | flops 1814175744 | bytes 69403312 | solution.py:21
  506.4 30.0 %convert_multiply_fusion = (bf16[1,1,2048,2304]{3,2,1,0:T(8,128)(2,1)}, bf16[1,1,2048,2304]{3,2,1,0:T(8,128)(2,1)}) fusion(f32[2048,2304]{1,0:T(8,128)} %fusion.182, f32[2048,2304]{1,0:T(8,128)} %get-tuple-element.264, bf16[2,2304,768]{2,1,0:T(8,128)(2,1)} %param.16, bf16[1,1,2048,768]{2,3,1,0:T(8,128)(2,1)} %fusion.202), kind=kOutput, calls=%fused_computation.170 | convolution fusion | flops 7323254784 | bytes 63307776 | tf_op jit(solution)/vmap(transpose(jvp()))/dot_general | solution.py:9
  536.4 105.4 %while.15 = (bf16[1,1,2048,768]{2,3,1,0:T(8,128)(2,1)}, bf16[1,1,2048,2304]{3,2,1,0:T(8,128)(2,1)}, f32[1,48,2304]{2,1,0:T(8,128)}, f32[1,48,2304]{2,1,0:T(8,128...) while((bf16[1,1,2048,768]{2,3,1,0:T(8,128)(2,1)}, ...), condition=%wide.windowed_dot_general_cond_rs.3.clone, body=%wide.windowed_dot_general_body_rs.3.clone.sunk | while | flops 1814175744 | bytes 91423392 | solution.py:21
  544.6 5.6 fusion.334
  571.4 5.6 fusion.334
  598.2 5.6 fusion.334
  625.0 5.6 fusion.334
  649.0 117.4 %while.12 = (bf16[1,1,2048,768]{2,3,1,0:T(8,128)(2,1)S(1)}, bf16[1,1,2048,2304]{3,2,1,0:T(8,128)(2,1)}, f32[1,48,2304]{2,1,0:T(8,128)}, f32[1,48,2304]{2,1,0:T(8...) while((bf16[1,1,2048,768]{2,3,1,0:T(8,128)(2,1)S(1)}, ...), condition=%wide.windowed_dot_general_cond_rs.clone, body=%wide.windowed_dot_general_body_rs.clone.sunk | while | flops 1814175744 | bytes 69403312 | solution.py:20
  669.1 8.9 collective-permute-done.2
  698.8 7.7 collective-permute-done.1
  724.9 5.5 fusion.310
  772.4 117.5 %while.13 = (bf16[1,1,2048,768]{2,3,1,0:T(8,128)(2,1)S(1)}, bf16[1,1,2048,2304]{3,2,1,0:T(8,128)(2,1)}, f32[1,48,2304]{2,1,0:T(8,128)}, f32[1,48,2304]{2,1,0:T(8...) while((bf16[1,1,2048,768]{2,3,1,0:T(8,128)(2,1)S(1)}, ...), condition=%wide.windowed_dot_general_cond_rs.1.clone, body=%wide.windowed_dot_general_body_rs.1.clone.sunk | while | flops 1814175744 | bytes 69403312 | solution.py:20
  780.9 5.5 fusion.318
  787.7 8.0 collective-permute-start.7
  810.0 9.3 collective-permute-start.5
  821.9 5.5 fusion.318
  899.7 51.7 %all-gather.10.cloned.1.call-done = bf16[1,2,768,2304]{3,2,1,0:T(8,128)(2,1)} async-done(((bf16[1,2,48,2304]{3,2,1,0:T(8,128)(2,1)}), bf16[1,2,768,2304]{3,2,1,0:T(8,128)(2,1)}) %all-gather.10.cloned.1.call-update) | async-done | bytes 7077904 | tf_op jit(solution)/reshape | solution.py:52
  951.4 6.6 copy.63
  957.9 6.6 copy.64
  (544 shorter events, 580.8 us)
Async XLA Ops:
  7.2 892.5 %all-gather.14.cloned.1.call-start = ((), (), s32[]{:S(2)}) async-start(), calls=%async_computation.2 | async-start | bytes 7520256 | tf_op jit(solution)/reshape | solution.py:52
  254.8 388.2 %collective-permute-start.28 = (f32[1,144,768]{2,1,0:T(8,128)}, f32[1,144,768]{2,1,0:T(8,128)}, u32[]{:S(2)}, u32[]{:S(2)}) collective-permute-start(f32[1,144,768]{2,1,0:T(8,128)} %get-tuple-element.45), channel_id=32, source_target_pairs={{0,1},{1,2},{2,3},{3,4},{4,5},{5,6},{6,7},{7,8},{8,9},{9,10},{10,1... | collective-permute-start | bytes 1327112 | tf_op jit(solution)/vmap(transpose(jvp()))/dot_general | solution.py:9
  400.6 243.7 %collective-permute-start.29 = (f32[1,144,768]{2,1,0:T(8,128)}, f32[1,144,768]{2,1,0:T(8,128)}, u32[]{:S(2)}, u32[]{:S(2)}) collective-permute-start(f32[1,144,768]{2,1,0:T(8,128)} %get-tuple-element.47), channel_id=38, source_target_pairs={{0,1},{1,2},{2,3},{3,4},{4,5},{5,6},{6,7},{7,8},{8,9},{9,10},{10,1... | collective-permute-start | bytes 1327112 | tf_op jit(solution)/vmap(transpose(jvp()))/dot_general | solution.py:9
  426.6 13.1 %collective-permute-start.8 = (f32[1,48,2304]{2,1,0:T(8,128)}, f32[1,48,2304]{2,1,0:T(8,128)}, u32[]{:S(2)}, u32[]{:S(2)}) collective-permute-start(f32[1,48,2304]{2,1,0:T(8,128)} %broadcast_select_fusion.28), channel_id=16, source_target_pairs={{0,1},{1,2},{2,3},{3,4},{4,5},{5,6},{6,7},{7,8},{8,9},{9,10},{10,1... | collective-permute-start | bytes 1327112 | tf_op jit(solution)/vmap(transpose(jvp()))/dot_general | solution.py:21
  452.0 13.6 %collective-permute-start.8 = (f32[1,48,2304]{2,1,0:T(8,128)}, f32[1,48,2304]{2,1,0:T(8,128)}, u32[]{:S(2)}, u32[]{:S(2)}) collective-permute-start(f32[1,48,2304]{2,1,0:T(8,128)} %broadcast_select_fusion.28), channel_id=16, source_target_pairs={{0,1},{1,2},{2,3},{3,4},{4,5},{5,6},{6,7},{7,8},{8,9},{9,10},{10,1... | collective-permute-start | bytes 1327112 | tf_op jit(solution)/vmap(transpose(jvp()))/dot_general | solution.py:21
  477.9 13.6 %collective-permute-start.8 = (f32[1,48,2304]{2,1,0:T(8,128)}, f32[1,48,2304]{2,1,0:T(8,128)}, u32[]{:S(2)}, u32[]{:S(2)}) collective-permute-start(f32[1,48,2304]{2,1,0:T(8,128)} %broadcast_select_fusion.28), channel_id=16, source_target_pairs={{0,1},{1,2},{2,3},{3,4},{4,5},{5,6},{6,7},{7,8},{8,9},{9,10},{10,1... | collective-permute-start | bytes 1327112 | tf_op jit(solution)/vmap(transpose(jvp()))/dot_general | solution.py:21
  479.7 11.8 %collective-permute-start.9 = (f32[1,48,2304]{2,1,0:T(8,128)}, f32[1,48,2304]{2,1,0:T(8,128)}, u32[]{:S(2)}, u32[]{:S(2)}) collective-permute-start(f32[1,48,2304]{2,1,0:T(8,128)} %broadcast_select_fusion.29), channel_id=15, source_target_pairs={{0,15},{1,0},{2,1},{3,2},{4,3},{5,4},{6,5},{7,6},{8,7},{9,8},{10,9... | collective-permute-start | bytes 1327112 | tf_op jit(solution)/vmap(transpose(jvp()))/dot_general | solution.py:21
  501.9 264.4 %collective-permute-start.26 = (f32[1,48,2304]{2,1,0:T(8,128)}, f32[1,48,2304]{2,1,0:T(8,128)}, u32[]{:S(2)}, u32[]{:S(2)}) collective-permute-start(f32[1,48,2304]{2,1,0:T(8,128)} %get-tuple-element.41), channel_id=19, source_target_pairs={{0,1},{1,2},{2,3},{3,4},{4,5},{5,6},{6,7},{7,8},{8,9},{9,10},{10,1... | collective-permute-start | bytes 1327112 | tf_op jit(solution)/vmap(transpose(jvp()))/dot_general | solution.py:21
  537.5 12.8 %collective-permute-start.12 = (f32[1,48,2304]{2,1,0:T(8,128)}, f32[1,48,2304]{2,1,0:T(8,128)}, u32[]{:S(2)}, u32[]{:S(2)}) collective-permute-start(f32[1,48,2304]{2,1,0:T(8,128)} %broadcast_select_fusion.30), channel_id=22, source_target_pairs={{0,1},{1,2},{2,3},{3,4},{4,5},{5,6},{6,7},{7,8},{8,9},{9,10},{10,1... | collective-permute-start | bytes 1327112 | tf_op jit(solution)/vmap(transpose(jvp()))/dot_general | solution.py:21
  563.2 13.8 %collective-permute-start.12 = (f32[1,48,2304]{2,1,0:T(8,128)}, f32[1,48,2304]{2,1,0:T(8,128)}, u32[]{:S(2)}, u32[]{:S(2)}) collective-permute-start(f32[1,48,2304]{2,1,0:T(8,128)} %broadcast_select_fusion.30), channel_id=22, source_target_pairs={{0,1},{1,2},{2,3},{3,4},{4,5},{5,6},{6,7},{7,8},{8,9},{9,10},{10,1... | collective-permute-start | bytes 1327112 | tf_op jit(solution)/vmap(transpose(jvp()))/dot_general | solution.py:21
  565.0 12.0 %collective-permute-start.13 = (f32[1,48,2304]{2,1,0:T(8,128)}, f32[1,48,2304]{2,1,0:T(8,128)}, u32[]{:S(2)}, u32[]{:S(2)}) collective-permute-start(f32[1,48,2304]{2,1,0:T(8,128)} %broadcast_select_fusion.31), channel_id=21, source_target_pairs={{0,15},{1,0},{2,1},{3,2},{4,3},{5,4},{6,5},{7,6},{8,7},{9,8},{10,9... | collective-permute-start | bytes 1327112 | tf_op jit(solution)/vmap(transpose(jvp()))/dot_general | solution.py:21
  590.0 13.8 %collective-permute-start.12 = (f32[1,48,2304]{2,1,0:T(8,128)}, f32[1,48,2304]{2,1,0:T(8,128)}, u32[]{:S(2)}, u32[]{:S(2)}) collective-permute-start(f32[1,48,2304]{2,1,0:T(8,128)} %broadcast_select_fusion.30), channel_id=22, source_target_pairs={{0,1},{1,2},{2,3},{3,4},{4,5},{5,6},{6,7},{7,8},{8,9},{9,10},{10,1... | collective-permute-start | bytes 1327112 | tf_op jit(solution)/vmap(transpose(jvp()))/dot_general | solution.py:21
  591.8 12.0 %collective-permute-start.13 = (f32[1,48,2304]{2,1,0:T(8,128)}, f32[1,48,2304]{2,1,0:T(8,128)}, u32[]{:S(2)}, u32[]{:S(2)}) collective-permute-start(f32[1,48,2304]{2,1,0:T(8,128)} %broadcast_select_fusion.31), channel_id=21, source_target_pairs={{0,15},{1,0},{2,1},{3,2},{4,3},{5,4},{6,5},{7,6},{8,7},{9,8},{10,9... | collective-permute-start | bytes 1327112 | tf_op jit(solution)/vmap(transpose(jvp()))/dot_general | solution.py:21
  616.8 13.8 %collective-permute-start.12 = (f32[1,48,2304]{2,1,0:T(8,128)}, f32[1,48,2304]{2,1,0:T(8,128)}, u32[]{:S(2)}, u32[]{:S(2)}) collective-permute-start(f32[1,48,2304]{2,1,0:T(8,128)} %broadcast_select_fusion.30), channel_id=22, source_target_pairs={{0,1},{1,2},{2,3},{3,4},{4,5},{5,6},{6,7},{7,8},{8,9},{9,10},{10,1... | collective-permute-start | bytes 1327112 | tf_op jit(solution)/vmap(transpose(jvp()))/dot_general | solution.py:21
  618.6 12.0 %collective-permute-start.13 = (f32[1,48,2304]{2,1,0:T(8,128)}, f32[1,48,2304]{2,1,0:T(8,128)}, u32[]{:S(2)}, u32[]{:S(2)}) collective-permute-start(f32[1,48,2304]{2,1,0:T(8,128)} %broadcast_select_fusion.31), channel_id=21, source_target_pairs={{0,15},{1,0},{2,1},{3,2},{4,3},{5,4},{6,5},{7,6},{8,7},{9,8},{10,9... | collective-permute-start | bytes 1327112 | tf_op jit(solution)/vmap(transpose(jvp()))/dot_general | solution.py:21
  641.8 125.9 %collective-permute-start.27 = (f32[1,48,2304]{2,1,0:T(8,128)}, f32[1,48,2304]{2,1,0:T(8,128)}, u32[]{:S(2)}, u32[]{:S(2)}) collective-permute-start(f32[1,48,2304]{2,1,0:T(8,128)} %get-tuple-element.43), channel_id=25, source_target_pairs={{0,1},{1,2},{2,3},{3,4},{4,5},{5,6},{6,7},{7,8},{8,9},{9,10},{10,1... | collective-permute-start | bytes 1327112 | tf_op jit(solution)/vmap(transpose(jvp()))/dot_general | solution.py:21
  648.9 250.8 %all-gather.12.cloned.1.call-start = ((), (), s32[]{:S(2)}) async-start(), calls=%async_computation.1 | async-start | bytes 7520256 | tf_op jit(solution)/reshape | solution.py:52
  649.8 12.4 %collective-permute-start = (f32[1,48,2304]{2,1,0:T(8,128)}, f32[1,48,2304]{2,1,0:T(8,128)}, u32[]{:S(2)}, u32[]{:S(2)}) collective-permute-start(f32[1,48,2304]{2,1,0:T(8,128)} %broadcast_select_fusion.24), channel_id=3, source_target_pairs={{0,1},{1,2},{2,3},{3,4},{4,5},{5,6},{6,7},{7,8},{8,9},{9,10},{10,1... | collective-permute-start | bytes 1327112 | tf_op jit(solution)/vmap(transpose(jvp()))/dot_general | solution.py:20
  663.4 14.5 %collective-permute-start.2 = (f32[1,48,2304]{2,1,0:T(8,128)S(1)}, f32[1,48,2304]{2,1,0:T(8,128)S(1)}, u32[]{:S(2)}, u32[]{:S(2)}) collective-permute-start(f32[1,48,2304]{2,1,0:T(8,128)S(1)} %get-tuple-element.455), channel_id=5, source_target_pairs={{0,1},{1,2},{2,3},{3,4},{4,5},{5,6},{6,7},{7,8},{8,9},{9,10},{10,1... | collective-permute-start | bytes 1327112 | tf_op jit(solution)/vmap(transpose(jvp()))/dot_general | solution.py:20
  663.5 18.2 %collective-permute-start.3 = (f32[1,48,2304]{2,1,0:T(8,128)S(1)}, f32[1,48,2304]{2,1,0:T(8,128)S(1)}, u32[]{:S(2)}, u32[]{:S(2)}) collective-permute-start(f32[1,48,2304]{2,1,0:T(8,128)S(1)} %get-tuple-element.456), channel_id=4, source_target_pairs={{0,15},{1,0},{2,1},{3,2},{4,3},{5,4},{6,5},{7,6},{8,7},{9,8},{10,9... | collective-permute-start | bytes 1327112 | tf_op jit(solution)/vmap(transpose(jvp()))/dot_general | solution.py:20
  684.5 14.2 %collective-permute-start = (f32[1,48,2304]{2,1,0:T(8,128)}, f32[1,48,2304]{2,1,0:T(8,128)}, u32[]{:S(2)}, u32[]{:S(2)}) collective-permute-start(f32[1,48,2304]{2,1,0:T(8,128)} %broadcast_select_fusion.24), channel_id=3, source_target_pairs={{0,1},{1,2},{2,3},{3,4},{4,5},{5,6},{6,7},{7,8},{8,9},{9,10},{10,1... | collective-permute-start | bytes 1327112 | tf_op jit(solution)/vmap(transpose(jvp()))/dot_general | solution.py:20
  686.3 20.1 %collective-permute-start.1 = (f32[1,48,2304]{2,1,0:T(8,128)}, f32[1,48,2304]{2,1,0:T(8,128)}, u32[]{:S(2)}, u32[]{:S(2)}) collective-permute-start(f32[1,48,2304]{2,1,0:T(8,128)} %broadcast_select_fusion.25), channel_id=2, source_target_pairs={{0,15},{1,0},{2,1},{3,2},{4,3},{5,4},{6,5},{7,6},{8,7},{9,8},{10,9... | collective-permute-start | bytes 1327112 | tf_op jit(solution)/vmap(transpose(jvp()))/dot_general | solution.py:20
  742.5 13.4 %collective-permute-start = (f32[1,48,2304]{2,1,0:T(8,128)}, f32[1,48,2304]{2,1,0:T(8,128)}, u32[]{:S(2)}, u32[]{:S(2)}) collective-permute-start(f32[1,48,2304]{2,1,0:T(8,128)} %broadcast_select_fusion.24), channel_id=3, source_target_pairs={{0,1},{1,2},{2,3},{3,4},{4,5},{5,6},{6,7},{7,8},{8,9},{9,10},{10,1... | collective-permute-start | bytes 1327112 | tf_op jit(solution)/vmap(transpose(jvp()))/dot_general | solution.py:20
  766.4 123.6 %collective-permute-start.24 = (f32[1,48,2304]{2,1,0:T(8,128)}, f32[1,48,2304]{2,1,0:T(8,128)}, u32[]{:S(2)}, u32[]{:S(2)}) collective-permute-start(f32[1,48,2304]{2,1,0:T(8,128)} %get-tuple-element.37), channel_id=6, source_target_pairs={{0,1},{1,2},{2,3},{3,4},{4,5},{5,6},{6,7},{7,8},{8,9},{9,10},{10,1... | collective-permute-start | bytes 1327112 | tf_op jit(solution)/vmap(transpose(jvp()))/dot_general | solution.py:20
  772.4 179.0 %all-gather.10.cloned.1.call-start = ((), (), s32[]{:S(2)}) async-start(), calls=%async_computation | async-start | bytes 7520256 | tf_op jit(solution)/reshape | solution.py:52
  773.7 12.6 %collective-permute-start.4 = (f32[1,48,2304]{2,1,0:T(8,128)}, f32[1,48,2304]{2,1,0:T(8,128)}, u32[]{:S(2)}, u32[]{:S(2)}) collective-permute-start(f32[1,48,2304]{2,1,0:T(8,128)} %broadcast_select_fusion.26), channel_id=9, source_target_pairs={{0,1},{1,2},{2,3},{3,4},{4,5},{5,6},{6,7},{7,8},{8,9},{9,10},{10,1... | collective-permute-start | bytes 1327112 | tf_op jit(solution)/vmap(transpose(jvp()))/dot_general | solution.py:20
  787.6 13.7 %collective-permute-start.6 = (f32[1,48,2304]{2,1,0:T(8,128)S(1)}, f32[1,48,2304]{2,1,0:T(8,128)S(1)}, u32[]{:S(2)}, u32[]{:S(2)}) collective-permute-start(f32[1,48,2304]{2,1,0:T(8,128)S(1)} %get-tuple-element.464), channel_id=11, source_target_pairs={{0,1},{1,2},{2,3},{3,4},{4,5},{5,6},{6,7},{7,8},{8,9},{9,10},{10,1... | collective-permute-start | bytes 1327112 | tf_op jit(solution)/vmap(transpose(jvp()))/dot_general | solution.py:20
  787.7 17.7 %collective-permute-start.7 = (f32[1,48,2304]{2,1,0:T(8,128)S(1)}, f32[1,48,2304]{2,1,0:T(8,128)S(1)}, u32[]{:S(2)}, u32[]{:S(2)}) collective-permute-start(f32[1,48,2304]{2,1,0:T(8,128)S(1)} %get-tuple-element.465), channel_id=10, source_target_pairs={{0,15},{1,0},{2,1},{3,2},{4,3},{5,4},{6,5},{7,6},{8,7},{9,8},{10,9... | collective-permute-start | bytes 1327112 | tf_op jit(solution)/vmap(transpose(jvp()))/dot_general | solution.py:20
  808.2 19.2 %collective-permute-start.4 = (f32[1,48,2304]{2,1,0:T(8,128)}, f32[1,48,2304]{2,1,0:T(8,128)}, u32[]{:S(2)}, u32[]{:S(2)}) collective-permute-start(f32[1,48,2304]{2,1,0:T(8,128)} %broadcast_select_fusion.26), channel_id=9, source_target_pairs={{0,1},{1,2},{2,3},{3,4},{4,5},{5,6},{6,7},{7,8},{8,9},{9,10},{10,1... | collective-permute-start | bytes 1327112 | tf_op jit(solution)/vmap(transpose(jvp()))/dot_general | solution.py:20
  810.0 19.0 %collective-permute-start.5 = (f32[1,48,2304]{2,1,0:T(8,128)}, f32[1,48,2304]{2,1,0:T(8,128)}, u32[]{:S(2)}, u32[]{:S(2)}) collective-permute-start(f32[1,48,2304]{2,1,0:T(8,128)} %broadcast_select_fusion.27), channel_id=8, source_target_pairs={{0,15},{1,0},{2,1},{3,2},{4,3},{5,4},{6,5},{7,6},{8,7},{9,8},{10,9... | collective-permute-start | bytes 1327112 | tf_op jit(solution)/vmap(transpose(jvp()))/dot_general | solution.py:20
  841.3 12.4 %collective-permute-start.4 = (f32[1,48,2304]{2,1,0:T(8,128)}, f32[1,48,2304]{2,1,0:T(8,128)}, u32[]{:S(2)}, u32[]{:S(2)}) collective-permute-start(f32[1,48,2304]{2,1,0:T(8,128)} %broadcast_select_fusion.26), channel_id=9, source_target_pairs={{0,1},{1,2},{2,3},{3,4},{4,5},{5,6},{6,7},{7,8},{8,9},{9,10},{10,1... | collective-permute-start | bytes 1327112 | tf_op jit(solution)/vmap(transpose(jvp()))/dot_general | solution.py:20
  865.9 13.6 %collective-permute-start.4 = (f32[1,48,2304]{2,1,0:T(8,128)}, f32[1,48,2304]{2,1,0:T(8,128)}, u32[]{:S(2)}, u32[]{:S(2)}) collective-permute-start(f32[1,48,2304]{2,1,0:T(8,128)} %broadcast_select_fusion.26), channel_id=9, source_target_pairs={{0,1},{1,2},{2,3},{3,4},{4,5},{5,6},{6,7},{7,8},{8,9},{9,10},{10,1... | collective-permute-start | bytes 1327112 | tf_op jit(solution)/vmap(transpose(jvp()))/dot_general | solution.py:20
  (136 other events, 1436.1 us)
Sparse Core Ops, SparseCore 0:
  649.0 60.0 all-gather.13
  772.5 56.3 all-gather.11
  899.8 51.5 all-gather.9
where the time goes:
time: 985 us; the launch traced here: 974 us
  matrix products  310 us (31%)
  other arithmetic  195 us (20%)
  waiting for transfers between devices  176 us (18%)
  starting transfers between devices  157 us (16%)
  local copies, waits for them, and re-layouts  73.4 us (7%)
  loops' own time  47.8 us (5%)
  between operations  14.9 us (2%)
    dot_general x19, matrix products, layer(): gate = jnp.dot(a, w['w_gate'], preferred_element_type=jnp.float32)  109 us
    dot_general x19, matrix products, matmul(): jnp.dot(a, w, preferred_element_type=jnp.float32).astype(jnp.bfloat16)  101 us
    dot_general x19, matrix products, layer(): up = jnp.dot(a, w['w_up'], preferred_element_type=jnp.float32)  99.9 us
    dot_general x60, other arithmetic  74.6 us
    dot_general x34, starting transfers between devices, layer(): gate = jnp.dot(a, w['w_gate'], preferred_element_type=jnp.float32)  61.3 us
    unnamed x47, local copies, waits for them, and re-layouts  58.5 us
    dot_general x34, waiting for transfers between devices, layer(): gate = jnp.dot(a, w['w_gate'], preferred_element_type=jnp.float32)  57.6 us
    dot_general x34, starting transfers between devices, layer(): up = jnp.dot(a, w['w_up'], preferred_element_type=jnp.float32)  54.4 us
  transfers between devices with their start and end apart: 105, of which 54 were waited for; matrix products, arithmetic and copies ran while one was open for 41% of the time, Pallas kernels for 0%

commit v1 on v0

v1 whole, which is shorter than its diff:
```python
import functools

import jax
import jax.numpy as jnp
from jax import lax
from jax.experimental import pallas as pl
from jax.experimental.pallas import tpu as pltpu
from jax.sharding import PartitionSpec as P

CORES = 2
F32, BF16 = jnp.float32, jnp.bfloat16
VMEM_LIMIT = 67_043_328


def dot(a, b):
    return lax.dot_general(a, b, (((1,), (0,)), ((), ())), preferred_element_type=F32)


def dot_nt(a, b):
    return lax.dot_general(a, b, (((1,), (1,)), ((), ())), preferred_element_type=F32)


def chain_kernel(layers, blocks, x_ref, dy_ref, wg_ref, wu_ref, wd_ref, left_ref, right_ref):
    d = x_ref.shape[1]
    per = wg_ref.shape[2] // d
    rows = d // blocks
    h = x_ref[...]
    saved = []
    for l in range(layers):
        wide = h.astype(F32)
        scale = lax.rsqrt(jnp.mean(wide * wide, -1, keepdims=True) + 1e-6)
        a = wide * scale
        left_ref[l, per] = a.T.astype(BF16)
        a = a.astype(BF16)
        gate = dot(a, wg_ref[l])
        up = dot(a, wu_ref[l])
        act = jax.nn.sigmoid(gate) * gate * up
        turned = act.T.astype(BF16)
        for j in range(blocks):
            for c in range(per):
                left_ref[l, c, j * rows : (j + 1) * rows, :] = turned[(j * per + c) * rows : (j * per + c + 1) * rows, :]
        saved.append((wide, scale, gate, up))
        if l < layers - 1:
            h = (wide + dot(act.astype(BF16), wd_ref[l]).astype(BF16).astype(F32)).astype(BF16)
    dh = dy_ref[...]
    for l in reversed(range(layers)):
        wide, scale, gate, up = saved[l]
        right_ref[l, 0] = dh
        dact = dot_nt(dh, wd_ref[l]).astype(BF16).astype(F32)
        sig = jax.nn.sigmoid(gate)
        silu = gate * sig
        dup = (dact * silu).astype(BF16)
        dgate = (dact * up * (sig + silu * (1.0 - sig))).astype(BF16)
        for c in range(per):
            right_ref[l, 1 + c] = dgate[:, c * d : (c + 1) * d]
            right_ref[l, 1 + per + c] = dup[:, c * d : (c + 1) * d]
        if l > 0:
            da = (dot_nt(dgate, wg_ref[l]) + dot_nt(dup, wu_ref[l])).astype(BF16).astype(F32)
            mean = jnp.mean(wide * da, -1, keepdims=True)
            dwide = da * scale - wide * (scale * scale * scale * mean)
            dh = (dh.astype(F32) + dwide.astype(BF16).astype(F32)).astype(BF16)


def chain(x, dy, wg, wu, wd, blocks, tile):
    layers, d, ff = wg.shape
    tokens = x.shape[0]
    per = ff // d
    whole = pl.BlockSpec(memory_space=pltpu.VMEM)
    tokens_by = pl.BlockSpec((tile, d), lambda t: (t, 0))
    return pl.pallas_call(
        functools.partial(chain_kernel, layers, blocks),
        grid=(tokens // tile,),
        in_specs=[tokens_by, tokens_by, whole, whole, whole],
        out_specs=[
            pl.BlockSpec((layers, per + 1, d, tile), lambda t: (0, 0, 0, t)),
            pl.BlockSpec((layers, 2 * per + 1, tile, d), lambda t: (0, 0, t, 0)),
        ],
        out_shape=[
            jax.ShapeDtypeStruct((layers, per + 1, d, tokens), BF16),
            jax.ShapeDtypeStruct((layers, 2 * per + 1, tokens, d), BF16),
        ],
        compiler_params=pltpu.CompilerParams(vmem_limit_bytes=VMEM_LIMIT, dimension_semantics=("arbitrary",)),
        name="chain",
    )(x, dy, wg, wu, wd)


def exchange_kernel(n, layers, per, wide, slots, *refs):
    (left_hbm, right_hbm, wd_hbm, wg_hbm, wu_hbm, *rest) = refs
    m_in, v_in, new_hbm, m_out, v_out = rest[0:3], rest[3:6], rest[6], rest[7:10], rest[10:13]
    (lbuf, rbuf, own, pair, got, w_rows, w_new, load_sem, w_sem, pair_send, pair_recv, sum_send, sum_recv,
     ring_send, ring_recv, side_send, side_recv, keep_sem) = rest[13:]
    weights = (wd_hbm, wg_hbm, wu_hbm)
    chips = n // CORES
    far = chips // 2
    near = chips - 1 - far
    d = rbuf.shape[2]
    rows = d // n
    per_layer = 3 * per
    chunks = layers * per_layer
    me = lax.axis_index("dp")
    z, k = lax.div(me, CORES), lax.rem(me, CORES)
    sign = 1 - 2 * k
    at = lambda chip: {"dp": lax.rem(chip + 2 * chips, chips) * CORES + k}
    place = lambda chip: lax.rem(chip + 2 * chips, chips)
    fore, back, mate = at(z + sign), at(z - sign), {"dp": z * CORES + 1 - k}

    def split(i):
        layer = layers - 1 - lax.div(i, per_layer)
        q = lax.rem(i, per_layer)
        kind = lax.div(q, per)
        inner = lax.div(kind + 1, 2)
        return layer, kind, lax.rem(q, per), (1 - inner) * q + inner * per, inner * (q - per + 1)

    def loads(i):
        layer, _, _, of_left, of_right = split(i)
        s = lax.rem(i, 2)
        return (
            pltpu.make_async_copy(left_hbm.at[layer, of_left], lbuf.at[s], load_sem.at[s, 0]),
            pltpu.make_async_copy(right_hbm.at[layer, of_right], rbuf.at[s], load_sem.at[s, 1]),
        )

    def remote(src, dst, send, recv, device):
        return pltpu.make_async_remote_copy(
            src_ref=src, dst_ref=dst, send_sem=send, recv_sem=recv, device_id=device, device_id_type=pl.DeviceIdType.MESH
        )

    def w_loads():
        return [
            pltpu.make_async_copy(w.at[:, pl.ds(pl.multiple_of(me * r.shape[1], rows), r.shape[1]), :], r, w_sem.at[j])
            for j, (w, r) in enumerate(zip(weights, w_rows, strict=True))
        ]

    for copy in loads(0):
        copy.start()
    for copy in w_loads():
        copy.start()
    barrier = pltpu.get_barrier_semaphore()
    for device in (fore, back, mate):
        pl.semaphore_signal(barrier, inc=1, device_id=device, device_id_type=pl.DeviceIdType.MESH)
    pl.semaphore_wait(barrier, 3)
    for copy in w_loads():
        copy.wait()

    def to_mate(i):
        return remote(own.at[lax.rem(i, slots), 1 - k], pair.at[i], pair_send.at[i], pair_recv.at[i], mate)

    def far_sum(i, s):
        return remote(pair.at[i, place(z - sign * (far - s))], got.at[i, s], sum_send.at[i, s], sum_recv.at[i, s], back)

    def near_sum(i, s):
        j = far + s
        return remote(pair.at[i, place(z + sign * (near - s))], got.at[i, j], sum_send.at[i, j], sum_recv.at[i, j], fore)

    def block(i, chip, core):
        return new_hbm.at[i, place(chip) * CORES + core]

    def far_ring(i, s):
        src = w_new.at[i] if s == 0 else block(i, z - sign * s, k)
        return remote(src, block(i, z - sign * s, k), ring_send.at[i, s], ring_recv.at[i, s], fore)

    def near_ring(i, s):
        src = w_new.at[i] if s == 0 else block(i, z + sign * s, k)
        return remote(src, block(i, z + sign * s, k), ring_send.at[i, far + s], ring_recv.at[i, far + s], back)

    def far_came(i, s):
        dst = block(i, z - sign * (s + 1), k)
        return remote(dst, dst, ring_send.at[i, s], ring_recv.at[i, s], fore)

    def near_came(i, s):
        dst = block(i, z + sign * (s + 1), k)
        return remote(dst, dst, ring_send.at[i, far + s], ring_recv.at[i, far + s], back)

    def side(i, j):
        offset = 0 if j == 0 else (-j if j <= far else j - far)
        src = w_new.at[i] if j == 0 else block(i, z + sign * offset, k)
        return remote(src, block(i, z + sign * offset, k), side_send.at[i, j], side_recv.at[i, j], mate)

    def side_came(i, j):
        offset = 0 if j == 0 else (-j if j <= far else j - far)
        dst = block(i, z - sign * offset, 1 - k)
        return remote(dst, dst, side_send.at[i, j], side_recv.at[i, j], mate)

    def keep(i):
        return pltpu.make_async_copy(w_new.at[i], block(i, z, k), keep_sem.at[i])

    def multiply(i):
        s, slot = lax.rem(i, 2), lax.rem(i, slots)

        @pl.when(i + 1 < chunks)
        def _():
            for copy in loads(i + 1):
                copy.start()

        for copy in loads(i):
            copy.wait()

        def columns(c, _):
            cut = pl.ds(pl.multiple_of(c * wide, wide), wide)
            out = dot(lbuf[s], rbuf[s, :, cut]).astype(BF16).reshape(chips, CORES, rows, wide)
            for core in range(CORES):
                own[slot, core, :, :, cut] = out[:, core]
            return 0

        lax.fori_loop(0, d // wide, columns, 0)
        to_mate(i).start()

    def total(i, chip, *others):
        j = place(chip)
        out = own[lax.rem(i, slots), k, j].astype(F32) + pair[i, j].astype(F32)
        for other in others:
            out = out + got[i, other].astype(F32)
        return out.astype(BF16)

    def first(i):
        to_mate(i).wait()
        pair[i, place(z - sign * far)] = total(i, z - sign * far)
        far_sum(i, 0).start()
        pair[i, place(z + sign * near)] = total(i, z + sign * near)
        near_sum(i, 0).start()

    def onward(s, i):
        far_sum(i, s - 1).wait_recv()
        pair[i, place(z - sign * (far - s))] = total(i, z - sign * (far - s), s - 1)
        far_sum(i, s).start()
        if s < near:
            near_sum(i, s - 1).wait_recv()
            pair[i, place(z + sign * (near - s))] = total(i, z + sign * (near - s), far + s - 1)
            near_sum(i, s).start()

    def update(i):
        far_sum(i, far - 1).wait_recv()
        near_sum(i, near - 1).wait_recv()
        g = total(i, z, far - 1, far + near - 1).astype(F32)
        layer, kind, part, _, _ = split(i)
        for which in range(3):

            @pl.when(kind == which)
            def _(which=which):
                if which == 0:
                    cut = (layer, pl.ds(pl.multiple_of(part * rows, rows), rows), slice(None))
                else:
                    cut = (layer, slice(None), pl.ds(pl.multiple_of(part * d, d), d))
                w = w_rows[which][cut].astype(F32)
                m = 0.9 * m_in[which][cut] + 0.1 * g
                v = 0.95 * v_in[which][cut] + 0.05 * g * g
                m_out[which][cut] = m
                v_out[which][cut] = v
                w_new[i] = (w - 0.02 * (m * lax.rsqrt(v + 1e-8) + 0.1 * w)).astype(BF16)

        far_ring(i, 0).start()
        near_ring(i, 0).start()
        side(i, 0).start()
        keep(i).start()

    def gather(s, i):
        far_came(i, s - 1).wait_recv()
        if s < far:
            far_ring(i, s).start()
        side(i, s).start()
        if s <= near:
            near_came(i, s - 1).wait_recv()
            if s < near:
                near_ring(i, s).start()
            side(i, far + s).start()

    def drain(i):
        for s in range(far):
            far_sum(i, s).wait_send()
            far_ring(i, s).wait_send()
        for s in range(near):
            near_sum(i, s).wait_send()
            near_ring(i, s).wait_send()
        for j in range(chips):
            side(i, j).wait_send()
            side_came(i, j).wait_recv()
        keep(i).wait()

    stages = [multiply, first]
    stages += [functools.partial(onward, s) for s in range(1, far)]
    stages += [update]
    stages += [functools.partial(gather, s) for s in range(1, far + 1)]
    stages += [drain]

    def tick(t, _):
        for offset in reversed(range(len(stages))):
            i = t - offset

            @pl.when((i >= 0) & (i < chunks))
            def _(i=i, stage=stages[offset]):
                stage(i)

        return 0

    lax.fori_loop(0, chunks + len(stages) - 1, tick, 0)


def exchange(left, right, weights, m, v, n):
    layers, _, d, tokens = left.shape
    per = left.shape[1] - 1
    rows = d // n
    chips = n // CORES
    hops = chips - 1
    chunks = layers * 3 * per
    stages = 4 + 2 * (chips // 2)
    slots = 2 + chips // 2 + 1
    wide = 256 if d % 256 == 0 else d
    anywhere, vmem = pl.BlockSpec(memory_space=pl.ANY), pl.BlockSpec(memory_space=pltpu.VMEM)
    sems = lambda *shape: pltpu.SemaphoreType.DMA(shape)
    return pl.pallas_call(
        functools.partial(exchange_kernel, n, layers, per, wide, slots),
        in_specs=[anywhere] * 5 + [vmem] * 6,
        out_specs=[anywhere] + [vmem] * 6,
        out_shape=[jax.ShapeDtypeStruct((chunks, n, rows, d), BF16), *(jax.ShapeDtypeStruct(t.shape, F32) for t in (*m, *v))],
        scratch_shapes=[
            pltpu.VMEM((2, d, tokens), BF16),
            pltpu.VMEM((2, tokens, d), BF16),
            pltpu.VMEM((slots, CORES, chips, rows, d), BF16),
            pltpu.VMEM((chunks, chips, rows, d), BF16),
            pltpu.VMEM((chunks, hops, rows, d), BF16),
            [pltpu.VMEM(t.shape, BF16) for t in m],
            pltpu.VMEM((chunks, rows, d), BF16),
            sems(2, 2),
            sems(3),
            sems(chunks),
            sems(chunks),
            sems(chunks, hops),
            sems(chunks, hops),
            sems(chunks, hops),
            sems(chunks, hops),
            sems(chunks, chips),
            sems(chunks, chips),
            sems(chunks),
        ],
        compiler_params=pltpu.CompilerParams(collective_id=0, has_side_effects=True, vmem_limit_bytes=VMEM_LIMIT),
        name="exchange",
    )(left, right, *weights, *m, *v)


def solution(mesh):
    n = mesh.shape["dp"]

    def of_a_device(x, dy, wg, wu, wd, mg, mu, md, vg, vu, vd):
        layers, d, ff = wg.shape
        per = ff // d
        tokens = x.shape[1]
        left, right = chain(x[0], dy[0], wg, wu, wd, n, min(tokens, 256))
        new, nmd, nmg, nmu, nvd, nvg, nvu = exchange(left, right, (wd, wg, wu), (md, mg, mu), (vd, vg, vu), n)
        new = new.reshape(layers, 3, per, n, d // n, d)[::-1]
        wide = lambda t: t.transpose(0, 2, 3, 1, 4).reshape(layers, d, ff)
        down = new[:, 0].transpose(0, 2, 1, 3, 4).reshape(layers, ff, d)
        return wide(new[:, 1]), wide(new[:, 2]), down, nmg, nmu, nmd, nvg, nvu, nvd

    data, whole, part, groups, both = P(("rep", "dp")), P(), P(None, "dp"), P("rep"), P("rep", "dp")
    return jax.shard_map(
        of_a_device,
        mesh=mesh,
        in_specs=(data, data, *[whole] * 3, *[part] * 6),
        out_specs=(*[groups] * 3, *[both] * 6),
        check_vma=False,
    )
```

time: 985 us -> 449 us (0.46)
  Pallas kernels: 0 us -> 335 us
  matrix products: 310 us -> 0 us
  other arithmetic: 195 us -> 0 us
  waiting for transfers between devices: 176 us -> 0 us
  starting transfers between devices: 157 us -> 0 us
  loops' own time: 47.8 us -> 0 us
  local copies, waits for them, and re-layouts: 73.4 us -> 112 us
  between operations: 14.9 us -> 0.7 us
    pallas_call x0 -> x2, Pallas kernels: none -> 335 us  [the longest x1 237 us: exchange(): pl.pallas_call(functools.partial(exchange_kernel, n, layers, per, wide, s...]
    dot_general x57 -> x0, matrix products: 310 us -> none  [the longest x19 109 us: layer(): gate = jnp.dot(a, w['w_gate'], preferred_element_type=jnp.float32)]
    dot_general x102 -> x0, starting transfers between devices: 157 us -> none  [the longest x34 61.3 us: layer(): gate = jnp.dot(a, w['w_gate'], preferred_element_type=jnp.float32)]
    dot_general x108 -> x0, other arithmetic: 149 us -> none
    dot_general x102 -> x0, waiting for transfers between devices: 125 us -> none  [the longest x34 57.6 us: layer(): gate = jnp.dot(a, w['w_gate'], preferred_element_type=jnp.float32)]
    reshape x3 -> x0, waiting for transfers between devices: 51.7 us -> none  [step(): t.reshape(-1, *t.shape[2:])]
    another operation x6 -> x0, loops' own time: 47.8 us -> none  [the longest x2 16.3 us: layer(): up = jnp.dot(a, w['w_up'], preferred_element_type=jnp.float32)]
    reshape x0 -> x2, local copies, waits for them, and re-layouts: none -> 38 us  [of_a_device(): wide = lambda t: t.transpose(0, 2, 3, 1, 4).reshape(layers, d, ff)]
  transfers between devices with their start and end apart: 105 -> 0, of which waited for: 54 -> 0; matrix products, arithmetic and copies ran while one was open for 41% -> 0% of each run, Pallas kernels for 0% -> 0%
where the time goes in v1:
time: 449 us; the launch traced here: 447 us
  Pallas kernels  335 us (75%)
  local copies, waits for them, and re-layouts  112 us (25%)
    pallas_call x1, Pallas kernels, exchange(): pl.pallas_call(functools.partial(exchange_kernel, n, layers, per, wide, s...  237 us
    pallas_call x1, Pallas kernels, chain(): pl.pallas_call(functools.partial(chain_kernel, layers, blocks), grid=(tok...  97.9 us
    unnamed x22, local copies, waits for them, and re-layouts  46 us
    reshape x2, local copies, waits for them, and re-layouts, of_a_device(): wide = lambda t: t.transpose(0, 2, 3, 1, 4).reshape(layers, d, ff)  38 us
    slice x1, local copies, waits for them, and re-layouts, of_a_device(): down = new[:, 0].transpose(0, 2, 1, 3, 4).reshape(layers, ff, d)  11.9 us
    transpose x2, local copies, waits for them, and re-layouts, of_a_device(): wide = lambda t: t.transpose(0, 2, 3, 1, 4).reshape(layers, d, ff)  11.3 us

profile of v1, /device:TPU:21, one launch (start us, length us, event | category | flops | bytes accessed | tf_op | source)
XLA Modules:
  0.0 447.5 jit_solution(4615280453498005070)
XLA Ops:
  0.6 97.9 %chain.1 = (bf16[2,4,768,2048]{3,2,1,0:T(8,128)(2,1)}, bf16[2,7,2048,768]{3,2,1,0:T(8,128)(2,1)}) custom-call(bf16[2048,768]{1,0:T(8,128)(2,1)} %bitcast.18, bf16[2048,768]{1,0:T(8,128)(2,1)} %bitcast.19, bf16[2,768,2304]{2,1,0:T(8,128)(2,1)} %refs_3_.1, bf16[2,768,2304]{2,1,0:T(8,128)(2,1)} %refs_4_.1, bf16[2,2304,768]{2,1,0:T(8,128)(2,1)} %refs_2_.1), custom_call_target="tpu_custom_call" | custom-call | tf_op jit(solution)/shard_map/chain/pallas_call | solution.py:70
  98.5 236.9 %exchange.1 = (bf16[18,16,48,768]{3,2,1,0:T(8,128)(2,1)}, f32[2,144,768]{2,1,0:T(8,128)}, f32[2,48,2304]{2,1,0:T(8,128)}, f32[2,48,2304]{2,1,0:T(8,128)}, f32[2,...) custom-call(bf16[2,4,768,2048]{3,2,1,0:T(8,128)(2,1)} %get-tuple-element.18.refs_0_, ...), custom_call_target="tpu_custom_call" | custom-call | tf_op jit(solution)/shard_map/exchange/pallas_call | solution.py:309
  335.4 11.9 %fusion = (bf16[2,1,3,16,48,768]{5,4,3,2,1,0:T(8,128)(2,1)S(1)}, bf16[2,1,3,16,48,768]{5,4,3,2,1,0:T(8,128)(2,1)}, bf16[2,1,3,16,48,768]{5,4,3,2,1,0:T(8,128)(2,1)}) fusion(bf16[2,3,3,16,48,768]{5,4,3,2,1,0:T(8,128)(2,1)} %bitcast.16), kind=kLoop, calls=%fused_computation.3 | loop fusion | bytes 42467328 | tf_op jit(solution)/shard_map/slice | solution.py:350
  347.3 0.8 reverse_bitcast_fusion.2
  348.1 0.0 copy-start
  348.1 4.1 copy.25
  352.2 1.5 copy-done
  353.7 28.5 %copy.26 = bf16[2,1,3,16,48,768]{5,2,4,3,0,1:T(4,128)(2,1)S(1)} copy(bf16[2,1,3,16,48,768]{5,4,3,2,1,0:T(8,128)(2,1)S(1)} %copy-done) | data formatting | bytes 14155776
  382.2 5.6 %reverse_bitcast_fusion.1 = bf16[2,16,48,3,768]{4,3,2,1,0:T(4,128)(2,1)} fusion(bf16[2,1,3,16,48,768]{5,2,4,3,0,1:T(4,128)(2,1)S(1)} %copy.26), kind=kLoop, calls=%fused_computation.1 | loop fusion | bytes 14155776 | tf_op jit(solution)/shard_map/transpose | solution.py:349
  387.8 18.9 %reshape.31 = bf16[2,768,2304]{2,1,0:T(8,128)(2,1)} reshape(bf16[2,16,48,3,768]{4,3,2,1,0:T(4,128)(2,1)} %reverse_bitcast_fusion.1) | data formatting | bytes 14155776 | tf_op jit(solution)/shard_map/reshape | solution.py:349
  406.7 10.6 %copy.27 = bf16[2,1,3,16,48,768]{5,2,4,3,0,1:T(4,128)(2,1)S(1)} copy(bf16[2,1,3,16,48,768]{5,4,3,2,1,0:T(8,128)(2,1)} %get-tuple-element.29) | data formatting | bytes 14155776
  417.3 5.6 %reverse_bitcast_fusion = bf16[2,16,48,3,768]{4,3,2,1,0:T(4,128)(2,1)} fusion(bf16[2,1,3,16,48,768]{5,2,4,3,0,1:T(4,128)(2,1)S(1)} %copy.27), kind=kLoop, calls=%fused_computation | loop fusion | bytes 14155776 | tf_op jit(solution)/shard_map/transpose | solution.py:349
  422.9 0.0 copy-start.6
  422.9 0.0 copy-start.5
  422.9 0.0 copy-start.4
  422.9 0.0 copy-start.3
  422.9 19.1 %reshape.32 = bf16[2,768,2304]{2,1,0:T(8,128)(2,1)} reshape(bf16[2,16,48,3,768]{4,3,2,1,0:T(4,128)(2,1)} %reverse_bitcast_fusion) | data formatting | bytes 14155776 | tf_op jit(solution)/shard_map/reshape | solution.py:349
  442.0 0.0 copy-done.6
  442.0 0.0 copy-start.2
  442.0 0.0 copy-start.1
  442.0 0.9 copy.34
  442.9 0.0 copy-done.5
  442.9 0.9 copy.35
  443.8 0.0 copy-done.4
  443.8 0.9 copy.36
  444.8 0.0 copy-done.3
  444.8 0.9 copy.37
  445.7 0.0 copy-done.2
  445.7 0.9 copy.38
  446.6 0.0 copy-done.1
  446.6 0.9 copy.39
Async XLA Ops:
  348.1 5.6 %copy-start = (bf16[2,1,3,16,48,768]{5,4,3,2,1,0:T(8,128)(2,1)S(1)}, bf16[2,1,3,16,48,768]{5,4,3,2,1,0:T(8,128)(2,1)}, u32[]{:S(2)}) copy-start(bf16[2,1,3,16,48,768]{5,4,3,2,1,0:T(8,128)(2,1)} %get-tuple-element.28) | copy-start | bytes 21233668
  422.9 19.1 %copy-start.6 = (f32[2,48,2304]{2,1,0:T(8,128)S(1)}, f32[2,48,2304]{2,1,0:T(8,128)}, u32[]{:S(2)}) copy-start(f32[2,48,2304]{2,1,0:T(8,128)} %get-tuple-element.42) | copy-start | bytes 2654212
  422.9 20.0 %copy-start.5 = (f32[2,48,2304]{2,1,0:T(8,128)S(1)}, f32[2,48,2304]{2,1,0:T(8,128)}, u32[]{:S(2)}) copy-start(f32[2,48,2304]{2,1,0:T(8,128)} %get-tuple-element.43) | copy-start | bytes 2654212
  422.9 20.9 %copy-start.4 = (f32[2,144,768]{2,1,0:T(8,128)S(1)}, f32[2,144,768]{2,1,0:T(8,128)}, u32[]{:S(2)}) copy-start(f32[2,144,768]{2,1,0:T(8,128)} %get-tuple-element.44) | copy-start | bytes 2654212
  422.9 21.8 %copy-start.3 = (f32[2,48,2304]{2,1,0:T(8,128)S(1)}, f32[2,48,2304]{2,1,0:T(8,128)}, u32[]{:S(2)}) copy-start(f32[2,48,2304]{2,1,0:T(8,128)} %get-tuple-element.45) | copy-start | bytes 2654212
  442.0 3.7 copy-start.2
  442.0 4.6 %copy-start.1 = (f32[2,144,768]{2,1,0:T(8,128)S(1)}, f32[2,144,768]{2,1,0:T(8,128)}, u32[]{:S(2)}) copy-start(f32[2,144,768]{2,1,0:T(8,128)} %get-tuple-element.47) | copy-start | bytes 2654212

commit v2 on v1

--- a/solution.py
+++ b/solution.py
@@ -20,12 +20,23 @@
     return lax.dot_general(a, b, (((1,), (1,)), ((), ())), preferred_element_type=F32)
 
 
-def chain_kernel(layers, blocks, x_ref, dy_ref, wg_ref, wu_ref, wd_ref, left_ref, right_ref):
+def silu_back(gate, up, dact):
+    sig = jax.nn.sigmoid(gate)
+    silu = gate * sig
+    return (dact * up * (sig + silu * (1.0 - sig))).astype(BF16), (dact * silu).astype(BF16)
+
+
+def adamw(w, m, v, g):
+    m = 0.9 * m + 0.1 * g
+    v = 0.95 * v + 0.05 * g * g
+    return (w - 0.02 * (m * lax.rsqrt(v + 1e-8) + 0.1 * w)).astype(BF16), m, v
+
+
+def chain_kernel(layers, blocks, x_ref, dy_ref, wg_ref, wu_ref, wd_ref, left_ref, right_ref, low_ref, h_ref):
     d = x_ref.shape[1]
     per = wg_ref.shape[2] // d
     rows = d // blocks
     h = x_ref[...]
-    saved = []
     for l in range(layers):
         wide = h.astype(F32)
         scale = lax.rsqrt(jnp.mean(wide * wide, -1, keepdims=True) + 1e-6)
@@ -39,26 +50,18 @@
         for j in range(blocks):
             for c in range(per):
                 left_ref[l, c, j * rows : (j + 1) * rows, :] = turned[(j * per + c) * rows : (j * per + c + 1) * rows, :]
-        saved.append((wide, scale, gate, up))
         if l < layers - 1:
+            for c in range(per):
+                low_ref[0, c] = gate[:, c * d : (c + 1) * d]
+                low_ref[1, c] = up[:, c * d : (c + 1) * d]
             h = (wide + dot(act.astype(BF16), wd_ref[l]).astype(BF16).astype(F32)).astype(BF16)
+            h_ref[...] = h
     dh = dy_ref[...]
-    for l in reversed(range(layers)):
-        wide, scale, gate, up = saved[l]
-        right_ref[l, 0] = dh
-        dact = dot_nt(dh, wd_ref[l]).astype(BF16).astype(F32)
-        sig = jax.nn.sigmoid(gate)
-        silu = gate * sig
-        dup = (dact * silu).astype(BF16)
-        dgate = (dact * up * (sig + silu * (1.0 - sig))).astype(BF16)
-        for c in range(per):
-            right_ref[l, 1 + c] = dgate[:, c * d : (c + 1) * d]
-            right_ref[l, 1 + per + c] = dup[:, c * d : (c + 1) * d]
-        if l > 0:
-            da = (dot_nt(dgate, wg_ref[l]) + dot_nt(dup, wu_ref[l])).astype(BF16).astype(F32)
-            mean = jnp.mean(wide * da, -1, keepdims=True)
-            dwide = da * scale - wide * (scale * scale * scale * mean)
-            dh = (dh.astype(F32) + dwide.astype(BF16).astype(F32)).astype(BF16)
+    right_ref[0] = dh
+    dgate, dup = silu_back(gate, up, dot_nt(dh, wd_ref[layers - 1]).astype(BF16).astype(F32))
+    for c in range(per):
+        right_ref[1 + c] = dgate[:, c * d : (c + 1) * d]
+        right_ref[1 + per + c] = dup[:, c * d : (c + 1) * d]
 
 
 def chain(x, dy, wg, wu, wd, blocks, tile):
@@ -73,22 +76,26 @@
         in_specs=[tokens_by, tokens_by, whole, whole, whole],
         out_specs=[
             pl.BlockSpec((layers, per + 1, d, tile), lambda t: (0, 0, 0, t)),
-            pl.BlockSpec((layers, 2 * per + 1, tile, d), lambda t: (0, 0, t, 0)),
+            pl.BlockSpec((2 * per + 1, tile, d), lambda t: (0, t, 0)),
+            pl.BlockSpec((2, per, tile, d), lambda t: (0, 0, t, 0)),
+            tokens_by,
         ],
         out_shape=[
             jax.ShapeDtypeStruct((layers, per + 1, d, tokens), BF16),
-            jax.ShapeDtypeStruct((layers, 2 * per + 1, tokens, d), BF16),
+            jax.ShapeDtypeStruct((2 * per + 1, tokens, d), BF16),
+            jax.ShapeDtypeStruct((2, per, tokens, d), F32),
+            jax.ShapeDtypeStruct((tokens, d), BF16),
         ],
         compiler_params=pltpu.CompilerParams(vmem_limit_bytes=VMEM_LIMIT, dimension_semantics=("arbitrary",)),
         name="chain",
     )(x, dy, wg, wu, wd)
 
 
-def exchange_kernel(n, layers, per, wide, slots, *refs):
-    (left_hbm, right_hbm, wd_hbm, wg_hbm, wu_hbm, *rest) = refs
-    m_in, v_in, new_hbm, m_out, v_out = rest[0:3], rest[3:6], rest[6], rest[7:10], rest[10:13]
-    (lbuf, rbuf, own, pair, got, w_rows, w_new, load_sem, w_sem, pair_send, pair_recv, sum_send, sum_recv,
-     ring_send, ring_recv, side_send, side_recv, keep_sem) = rest[13:]
+def exchange_kernel(n, layers, per, wide, slots, tile, early, *refs):
+    (left_hbm, top_hbm, low_hbm, h_hbm, wd_hbm, wg_hbm, wu_hbm, *rest) = refs
+    m_hbm, v_hbm, new_hbm, g_out, right_hbm = rest[0:3], rest[3:6], rest[6], rest[7], rest[8]
+    (lbuf, rbuf, own, pair, got, state, w_new, w_tile, t_tile, g_tile, s_tile, load_sem, state_sem, pair_send, pair_recv,
+     sum_send, sum_recv, ring_send, ring_recv, side_send, side_recv, keep_sem, w_sem, in_sem, out_sem) = rest[9:]
     weights = (wd_hbm, wg_hbm, wu_hbm)
     chips = n // CORES
     far = chips // 2
@@ -111,35 +118,157 @@
         inner = lax.div(kind + 1, 2)
         return layer, kind, lax.rem(q, per), (1 - inner) * q + inner * per, inner * (q - per + 1)
 
-    def loads(i):
+    def start_loads(i):
         layer, _, _, of_left, of_right = split(i)
         s = lax.rem(i, 2)
-        return (
-            pltpu.make_async_copy(left_hbm.at[layer, of_left], lbuf.at[s], load_sem.at[s, 0]),
-            pltpu.make_async_copy(right_hbm.at[layer, of_right], rbuf.at[s], load_sem.at[s, 1]),
-        )
+        pltpu.make_async_copy(left_hbm.at[layer, of_left], lbuf.at[s], load_sem.at[s, 0]).start()
+        for low, right in enumerate((top_hbm, right_hbm)):
+
+            @pl.when((i >= per_layer) == (low == 1))
+            def _(right=right):
+                pltpu.make_async_copy(right.at[of_right], rbuf.at[s], load_sem.at[s, 1]).start()
+
+    def wait_loads(i):
+        s = lax.rem(i, 2)
+        pltpu.make_async_copy(left_hbm.at[0, 0], lbuf.at[s], load_sem.at[s, 0]).wait()
+        pltpu.make_async_copy(top_hbm.at[0], rbuf.at[s], load_sem.at[s, 1]).wait()
+
+    def start_state(i):
+        layer, kind, part, _, _ = split(i)
+        s = lax.rem(i, 2)
+        for which in range(3):
+
+            @pl.when(kind == which)
+            def _(which=which):
+                if which == 0:
+                    first_row = pl.multiple_of(me * (per * rows) + part * rows, rows)
+                    w_cut = (layer, pl.ds(first_row, rows), slice(None))
+                    cut = (layer, pl.ds(pl.multiple_of(part * rows, rows), rows), slice(None))
+                else:
+                    columns = pl.ds(pl.multiple_of(part * d, d), d)
+                    w_cut = (layer, pl.ds(pl.multiple_of(me * rows, rows), rows), columns)
+                    cut = (layer, slice(None), columns)
+                pltpu.make_async_copy(weights[which].at[w_cut], w_new.at[i], state_sem.at[s, 0]).start()
+                pltpu.make_async_copy(m_hbm[which].at[cut], state.at[s, 0], state_sem.at[s, 1]).start()
+                pltpu.make_async_copy(v_hbm[which].at[cut], state.at[s, 1], state_sem.at[s, 2]).start()
+
+    def wait_state(i):
+        s = lax.rem(i, 2)
+        pltpu.make_async_copy(wg_hbm.at[0, 0:rows, 0:d], w_new.at[i], state_sem.at[s, 0]).wait()
+        for j, moment in enumerate((m_hbm[1], v_hbm[1])):
+            pltpu.make_async_copy(moment.at[0, :, 0:d], state.at[s, j], state_sem.at[s, 1 + j]).wait()
 
     def remote(src, dst, send, recv, device):
         return pltpu.make_async_remote_copy(
             src_ref=src, dst_ref=dst, send_sem=send, recv_sem=recv, device_id=device, device_id_type=pl.DeviceIdType.MESH
         )
 
-    def w_loads():
+    tiles = top_hbm.shape[1] // tile
+
+    def tokens_of(e):
+        return pl.ds(pl.multiple_of(lax.rem(e, tiles) * tile, tile), tile)
+
+    def top_weights():
         return [
-            pltpu.make_async_copy(w.at[:, pl.ds(pl.multiple_of(me * r.shape[1], rows), r.shape[1]), :], r, w_sem.at[j])
-            for j, (w, r) in enumerate(zip(weights, w_rows, strict=True))
+            pltpu.make_async_copy(w.at[layers - 1, :, c * d : (c + 1) * d], w_tile.at[j * per + c], w_sem.at[j * per + c])
+            for j, w in enumerate((wg_hbm, wu_hbm))
+            for c in range(per)
         ]
 
-    for copy in loads(0):
-        copy.start()
-    for copy in w_loads():
+    def low_weights():
+        return [pltpu.make_async_copy(wd_hbm.at[0, c * d : (c + 1) * d, :], w_tile.at[c], w_sem.at[c]) for c in range(per)]
+
+    def top_inputs(e):
+        cut = tokens_of(e)
+        return (
+            pltpu.make_async_copy(top_hbm.at[1:, cut, :], t_tile, in_sem.at[0]),
+            pltpu.make_async_copy(top_hbm.at[0, cut, :], s_tile.at[0], in_sem.at[1]),
+            pltpu.make_async_copy(h_hbm.at[cut, :], s_tile.at[1], in_sem.at[2]),
+        )
+
+    def low_inputs(e):
+        cut = tokens_of(e)
+        return (
+            pltpu.make_async_copy(low_hbm.at[:, :, cut, :], g_tile, in_sem.at[3]),
+            pltpu.make_async_copy(right_hbm.at[0, cut, :], s_tile.at[0], in_sem.at[1]),
+        )
+
+    def top_result(e):
+        return pltpu.make_async_copy(s_tile.at[2], right_hbm.at[0, tokens_of(e), :], out_sem.at[0])
+
+    def low_result(e):
+        return pltpu.make_async_copy(t_tile, right_hbm.at[1:, tokens_of(e), :], out_sem.at[1])
+
+    def extra(e):
+        @pl.when((e >= 0) & (e < tiles))
+        def _():
+            @pl.when(e == 0)
+            def _():
+                for copy in top_weights():
+                    copy.wait()
+
+            @pl.when(e > 0)
+            def _():
+                top_result(e - 1).wait()
+
+            for copy in top_inputs(e):
+                copy.wait()
+            da = dot_nt(t_tile[0], w_tile[0])
+            for c in range(1, 2 * per):
+                da = da + dot_nt(t_tile[c], w_tile[c])
+            da = da.astype(BF16).astype(F32)
+            wide = s_tile[1].astype(F32)
+            scale = lax.rsqrt(jnp.mean(wide * wide, -1, keepdims=True) + 1e-6)
+            mean = jnp.mean(wide * da, -1, keepdims=True)
+            dwide = da * scale - wide * (scale * scale * scale * mean)
+            s_tile[2] = (s_tile[0].astype(F32) + dwide.astype(BF16).astype(F32)).astype(BF16)
+            top_result(e).start()
+
+            @pl.when(e < tiles - 1)
+            def _():
+                for copy in top_inputs(e + 1):
+                    copy.start()
+
+            @pl.when(e == tiles - 1)
+            def _():
+                for copy in (*low_weights(), *low_inputs(e + 1)):
+                    copy.start()
+
+        @pl.when((e >= tiles) & (e < 2 * tiles))
+        def _():
+            @pl.when(e == tiles)
+            def _():
+                top_result(e - 1).wait()
+                for copy in low_weights():
+                    copy.wait()
+
+            @pl.when(e > tiles)
+            def _():
+                low_result(e - 1).wait()
+
+            for copy in low_inputs(e):
+                copy.wait()
+            for c in range(per):
+                dact = dot_nt(s_tile[0], w_tile[c]).astype(BF16).astype(F32)
+                t_tile[c], t_tile[per + c] = silu_back(g_tile[0, c], g_tile[1, c], dact)
+            low_result(e).start()
+
+            @pl.when(e < 2 * tiles - 1)
+            def _():
+                for copy in low_inputs(e + 1):
+                    copy.start()
+
+        @pl.when(e == 2 * tiles)
+        def _():
+            low_result(e - 1).wait()
+
+    start_loads(0)
+    for copy in (*top_weights(), *top_inputs(0)):
         copy.start()
     barrier = pltpu.get_barrier_semaphore()
     for device in (fore, back, mate):
         pl.semaphore_signal(barrier, inc=1, device_id=device, device_id_type=pl.DeviceIdType.MESH)
     pl.semaphore_wait(barrier, 3)
-    for copy in w_loads():
-        copy.wait()
 
     def to_mate(i):
         return remote(own.at[lax.rem(i, slots), 1 - k], pair.at[i], pair_send.at[i], pair_recv.at[i], mate)
@@ -188,11 +317,9 @@
 
         @pl.when(i + 1 < chunks)
         def _():
-            for copy in loads(i + 1):
-                copy.start()
-
-        for copy in loads(i):
-            copy.wait()
+            start_loads(i + 1)
+
+        wait_loads(i)
 
         def columns(c, _):
             cut = pl.ds(pl.multiple_of(c * wide, wide), wide)
@@ -226,27 +353,18 @@
             near_sum(i, s - 1).wait_recv()
             pair[i, place(z + sign * (near - s))] = total(i, z + sign * (near - s), far + s - 1)
             near_sum(i, s).start()
+        if s == far - 1:
+            start_state(i)
 
     def update(i):
         far_sum(i, far - 1).wait_recv()
         near_sum(i, near - 1).wait_recv()
-        g = total(i, z, far - 1, far + near - 1).astype(F32)
-        layer, kind, part, _, _ = split(i)
-        for which in range(3):
-
-            @pl.when(kind == which)
-            def _(which=which):
-                if which == 0:
-                    cut = (layer, pl.ds(pl.multiple_of(part * rows, rows), rows), slice(None))
-                else:
-                    cut = (layer, slice(None), pl.ds(pl.multiple_of(part * d, d), d))
-                w = w_rows[which][cut].astype(F32)
-                m = 0.9 * m_in[which][cut] + 0.1 * g
-                v = 0.95 * v_in[which][cut] + 0.05 * g * g
-                m_out[which][cut] = m
-                v_out[which][cut] = v
-                w_new[i] = (w - 0.02 * (m * lax.rsqrt(v + 1e-8) + 0.1 * w)).astype(BF16)
-
+        g = total(i, z, far - 1, far + near - 1)
+        g_out[i] = g
+        g = g.astype(F32)
+        wait_state(i)
+        s = lax.rem(i, 2)
+        w_new[i] = adamw(w_new[i].astype(F32), state[s, 0], state[s, 1], g)[0]
         far_ring(i, 0).start()
         near_ring(i, 0).start()
         side(i, 0).start()
@@ -289,38 +407,49 @@
             def _(i=i, stage=stages[offset]):
                 stage(i)
 
+            if offset == far + 1:
+                extra(2 * (t - early))
+        extra(2 * (t - early) + 1)
         return 0
 
     lax.fori_loop(0, chunks + len(stages) - 1, tick, 0)
 
 
-def exchange(left, right, weights, m, v, n):
+def exchange(left, top, low, h, weights, m, v, n):
     layers, _, d, tokens = left.shape
     per = left.shape[1] - 1
     rows = d // n
     chips = n // CORES
     hops = chips - 1
     chunks = layers * 3 * per
-    stages = 4 + 2 * (chips // 2)
-    slots = 2 + chips // 2 + 1
+    tile = min(tokens, 256)
     wide = 256 if d % 256 == 0 else d
     anywhere, vmem = pl.BlockSpec(memory_space=pl.ANY), pl.BlockSpec(memory_space=pltpu.VMEM)
     sems = lambda *shape: pltpu.SemaphoreType.DMA(shape)
+    slots = chips // 2 + 2
     return pl.pallas_call(
-        functools.partial(exchange_kernel, n, layers, per, wide, slots),
-        in_specs=[anywhere] * 5 + [vmem] * 6,
-        out_specs=[anywhere] + [vmem] * 6,
-        out_shape=[jax.ShapeDtypeStruct((chunks, n, rows, d), BF16), *(jax.ShapeDtypeStruct(t.shape, F32) for t in (*m, *v))],
+        functools.partial(exchange_kernel, n, layers, per, wide, slots, tile, 3),
+        in_specs=[anywhere] * 13,
+        out_specs=[anywhere, vmem, anywhere],
+        out_shape=[
+            jax.ShapeDtypeStruct((chunks, n, rows, d), BF16),
+            jax.ShapeDtypeStruct((chunks, rows, d), BF16),
+            jax.ShapeDtypeStruct((2 * per + 1, tokens, d), BF16),
+        ],
         scratch_shapes=[
             pltpu.VMEM((2, d, tokens), BF16),
             pltpu.VMEM((2, tokens, d), BF16),
             pltpu.VMEM((slots, CORES, chips, rows, d), BF16),
             pltpu.VMEM((chunks, chips, rows, d), BF16),
             pltpu.VMEM((chunks, hops, rows, d), BF16),
-            [pltpu.VMEM(t.shape, BF16) for t in m],
+            pltpu.VMEM((2, 2, rows, d), F32),
             pltpu.VMEM((chunks, rows, d), BF16),
+            pltpu.VMEM((2 * per, d, d), BF16),
+            pltpu.VMEM((2 * per, tile, d), BF16),
+            pltpu.VMEM((2, per, tile, d), F32),
+            pltpu.VMEM((3, tile, d), BF16),
             sems(2, 2),
-            sems(3),
+            sems(2, 3),
             sems(chunks),
             sems(chunks),
             sems(chunks, hops),
@@ -330,10 +459,47 @@
             sems(chunks, chips),
             sems(chunks, chips),
             sems(chunks),
+            sems(2 * per),
+            sems(4),
+            sems(2),
         ],
         compiler_params=pltpu.CompilerParams(collective_id=0, has_side_effects=True, vmem_limit_bytes=VMEM_LIMIT),
         name="exchange",
-    )(left, right, *weights, *m, *v)
+    )(left, top, low, h, *weights, *m, *v)
+
+
+def unpack_kernel(*refs):
+    chunks, sums, m_in, v_in = refs[0:3], refs[3:6], refs[6:9], refs[9:12]
+    (down_out, gate_out, up_out), m_out, v_out = refs[12:15], refs[15:18], refs[18:21]
+    down_out[0, :, 0] = chunks[0][0]
+    gate_out[0] = chunks[1][0].reshape(gate_out.shape[1:])
+    up_out[0] = chunks[2][0].reshape(up_out.shape[1:])
+    for kind in range(3):
+        _, m_out[kind][...], v_out[kind][...] = adamw(0.0, m_in[kind][...], v_in[kind][...], sums[kind][...].astype(F32))
+
+
+def unpack(new, g, m, v, shape, n):
+    layers, d, ff = shape
+    per, rows = ff // d, d // n
+    number = lambda l, c, kind: (layers - 1 - l) * 3 * per + kind * per + c
+    chunk = lambda kind: pl.BlockSpec((1, n, rows, d), lambda l, c: (number(l, c, kind), 0, 0, 0))
+    sums = lambda kind: pl.BlockSpec((1, rows, d), lambda l, c: (number(l, c, kind), 0, 0))
+    wide = lambda height: pl.BlockSpec((1, height, d), lambda l, c: (l, 0, c))
+    moments = [pl.BlockSpec((1, rows, d), lambda l, c: (l, c, 0)), wide(rows), wide(rows)] * 2
+    down, *rest = pl.pallas_call(
+        unpack_kernel,
+        grid=(layers, per),
+        in_specs=[*(chunk(kind) for kind in range(3)), *(sums(kind) for kind in range(3)), *moments],
+        out_specs=[pl.BlockSpec((1, n, 1, rows, d), lambda l, c: (l, 0, c, 0, 0)), wide(d), wide(d), *moments],
+        out_shape=[
+            jax.ShapeDtypeStruct((layers, n, per, rows, d), BF16),
+            *[jax.ShapeDtypeStruct((layers, d, ff), BF16)] * 2,
+            *(jax.ShapeDtypeStruct(t.shape, F32) for t in (*m, *v)),
+        ],
+        compiler_params=pltpu.CompilerParams(vmem_limit_bytes=VMEM_LIMIT),
+        name="unpack",
+    )(new, new, new, g, g, g, *m, *v)
+    return down.reshape(layers, ff, d), *rest
 
 
 def solution(mesh):
@@ -341,14 +507,12 @@
 
     def of_a_device(x, dy, wg, wu, wd, mg, mu, md, vg, vu, vd):
         layers, d, ff = wg.shape
-        per = ff // d
         tokens = x.shape[1]
-        left, right = chain(x[0], dy[0], wg, wu, wd, n, min(tokens, 256))
-        new, nmd, nmg, nmu, nvd, nvg, nvu = exchange(left, right, (wd, wg, wu), (md, mg, mu), (vd, vg, vu), n)
-        new = new.reshape(layers, 3, per, n, d // n, d)[::-1]
-        wide = lambda t: t.transpose(0, 2, 3, 1, 4).reshape(layers, d, ff)
-        down = new[:, 0].transpose(0, 2, 1, 3, 4).reshape(layers, ff, d)
-        return wide(new[:, 1]), wide(new[:, 2]), down, nmg, nmu, nmd, nvg, nvu, nvd
+        left, top, low, h = chain(x[0], dy[0], wg, wu, wd, n, min(tokens, 256))
+        m, v = (md, mg, mu), (vd, vg, vu)
+        new, g, _ = exchange(left, top, low, h, (wd, wg, wu), m, v, n)
+        down, gate, up, md, mg, mu, vd, vg, vu = unpack(new, g, m, v, (layers, d, ff), n)
+        return gate, up, down, mg, mu, md, vg, vu, vd
 
     data, whole, part, groups, both = P(("rep", "dp")), P(), P(None, "dp"), P("rep"), P("rep", "dp")
     return jax.shard_map(

time: 449 us -> 333 us (0.74)
  local copies, waits for them, and re-layouts: 112 us -> 0 us
    unnamed x22 -> x0, local copies, waits for them, and re-layouts: 46 us -> none
    reshape x2 -> x0, local copies, waits for them, and re-layouts: 38 us -> none  [of_a_device(): wide = lambda t: t.transpose(0, 2, 3, 1, 4).reshape(layers, d, ff)]
    pallas_call x1, Pallas kernels: 97.9 us -> 67.3 us  [chain(): pl.pallas_call(functools.partial(chain_kernel, layers, blocks), grid=(tok...]
    pallas_call x0 -> x1, Pallas kernels: none -> 17.9 us  [unpack(): pl.pallas_call(unpack_kernel, grid=(layers, per), in_specs=[*(chunk(kind)...]
    transpose x4 -> x0, local copies, waits for them, and re-layouts: 16.1 us -> none  [the longest x2 11.3 us: of_a_device(): wide = lambda t: t.transpose(0, 2, 3, 1, 4).reshape(layers, d, ff)]
    slice x1 -> x0, local copies, waits for them, and re-layouts: 11.9 us -> none  [of_a_device(): down = new[:, 0].transpose(0, 2, 1, 3, 4).reshape(layers, ff, d)]
    pallas_call x1, Pallas kernels: 237 us -> 247 us  [exchange(): pl.pallas_call(functools.partial(exchange_kernel, n, layers, per, wide, s...]
where the time goes in v2:
time: 333 us
  Pallas kernels  332 us (100%)
    pallas_call x1, Pallas kernels, exchange(): pl.pallas_call(functools.partial(exchange_kernel, n, layers, per, wide, s...  247 us
    pallas_call x1, Pallas kernels, chain(): pl.pallas_call(functools.partial(chain_kernel, layers, blocks), grid=(tok...  67.3 us
    pallas_call x1, Pallas kernels, unpack(): pl.pallas_call(unpack_kernel, grid=(layers, per), in_specs=[*(chunk(kind)...  17.9 us

profile of v2, /device:TPU:21, one launch (start us, length us, event | category | flops | bytes accessed | tf_op | source)
XLA Modules:
  0.0 332.7 jit_solution(4214018310302813018)
XLA Ops:
  0.6 67.3 %chain.1 = (bf16[2,4,768,2048]{3,2,1,0:T(8,128)(2,1)}, bf16[7,2048,768]{2,1,0:T(8,128)(2,1)}, f32[2,3,2048,768]{3,2,1,0:T(8,128)}, bf16[2048,768]{1,0:T(8,128)(2,1)}) custom-call(bf16[2048,768]{1,0:T(8,128)(2,1)} %bitcast.3, bf16[2048,768]{1,0:T(8,128)(2,1)} %bitcast.4, bf16[2,768,2304]{2,1,0:T(8,128)(2,1)} %refs_5_.1, bf16[2,768,2304]{2,1,0:T(8,128)(2,1)} %refs_6_.2, ...), custom_call_target="tpu_custom_call" | custom-call | tf_op jit(solution)/shard_map/chain/pallas_call | solution.py:73
  67.9 246.8 %exchange.1 = (bf16[18,16,48,768]{3,2,1,0:T(8,128)(2,1)}, bf16[18,48,768]{2,1,0:T(8,128)(2,1)}, bf16[7,2048,768]{2,1,0:T(8,128)(2,1)}) custom-call(bf16[2,4,768,2048]{3,2,1,0:T(8,128)(2,1)} %get-tuple-element.24.refs_0_, bf16[7,2048,768]{2,1,0:T(8,128)(2,1)} %get-tuple-element.25.refs_1_, f32[2,3,2048,768]{3,2,1,0:T(8,128)} %get-tuple-element.26.refs_2_, ...), custom_call_target="tpu_custom_call" | custom-call | tf_op jit(solution)/shard_map/exchange/pallas_call | solution.py:430
  314.7 17.9 %unpack.1 = (bf16[2,16,3,48,768]{4,3,2,1,0:T(8,128)(2,1)}, bf16[2,768,2304]{2,1,0:T(8,128)(2,1)}, bf16[2,768,2304]{2,1,0:T(8,128)(2,1)}, f32[2,144,768]{2,1,0:T(...) custom-call(bf16[18,16,48,768]{3,2,1,0:T(8,128)(2,1)} %get-tuple-ele, ...), custom_call_target="tpu_custom_call" | custom-call | tf_op jit(solution)/shard_map/unpack/pallas_call | solution.py:489

commit v3 on v2

--- a/solution.py
+++ b/solution.py
@@ -32,48 +32,72 @@
     return (w - 0.02 * (m * lax.rsqrt(v + 1e-8) + 0.1 * w)).astype(BF16), m, v
 
 
-def chain_kernel(layers, blocks, x_ref, dy_ref, wg_ref, wu_ref, wd_ref, left_ref, right_ref, low_ref, h_ref):
+def chain_kernel(layers, blocks, x_ref, dy_ref, *refs):
+    weights_hbm, (left_ref, right_ref, low_ref, h_ref), weights, sem = refs[:3], refs[3:7], refs[7:10], refs[10]
+    wg_ref, wu_ref, wd_ref = weights
     d = x_ref.shape[1]
     per = wg_ref.shape[2] // d
     rows = d // blocks
-    h = x_ref[...]
-    for l in range(layers):
-        wide = h.astype(F32)
-        scale = lax.rsqrt(jnp.mean(wide * wide, -1, keepdims=True) + 1e-6)
-        a = wide * scale
-        left_ref[l, per] = a.T.astype(BF16)
-        a = a.astype(BF16)
-        gate = dot(a, wg_ref[l])
-        up = dot(a, wu_ref[l])
-        act = jax.nn.sigmoid(gate) * gate * up
-        turned = act.T.astype(BF16)
-        for j in range(blocks):
+
+    def fetch(l, which):
+        return pltpu.make_async_copy(weights_hbm[which].at[l], weights[which].at[l], sem.at[l, which])
+
+    def body(at_first):
+        wait = lambda l, which: fetch(l, which).wait() if at_first else None
+        if at_first:
+            for l in range(layers):
+                for which in range(3):
+                    fetch(l, which).start()
+        h = x_ref[...]
+        for l in range(layers):
+            wide = h.astype(F32)
+            scale = lax.rsqrt(jnp.mean(wide * wide, -1, keepdims=True) + 1e-6)
+            a = wide * scale
+            left_ref[l, per] = a.T.astype(BF16)
+            a = a.astype(BF16)
+            wait(l, 0)
+            wait(l, 1)
+            parts, out = [], None
             for c in range(per):
-                left_ref[l, c, j * rows : (j + 1) * rows, :] = turned[(j * per + c) * rows : (j * per + c + 1) * rows, :]
-        if l < layers - 1:
-            for c in range(per):
-                low_ref[0, c] = gate[:, c * d : (c + 1) * d]
-                low_ref[1, c] = up[:, c * d : (c + 1) * d]
-            h = (wide + dot(act.astype(BF16), wd_ref[l]).astype(BF16).astype(F32)).astype(BF16)
-            h_ref[...] = h
-    dh = dy_ref[...]
-    right_ref[0] = dh
-    dgate, dup = silu_back(gate, up, dot_nt(dh, wd_ref[layers - 1]).astype(BF16).astype(F32))
-    for c in range(per):
-        right_ref[1 + c] = dgate[:, c * d : (c + 1) * d]
-        right_ref[1 + per + c] = dup[:, c * d : (c + 1) * d]
+                cut = slice(c * d, (c + 1) * d)
+                gate, up = dot(a, wg_ref[l, :, cut]), dot(a, wu_ref[l, :, cut])
+                act = jax.nn.sigmoid(gate) * gate * up
+                turned = act.T.astype(BF16)
+                for g in range(blocks):
+                    j, p = divmod(c * blocks + g, per)
+                    left_ref[l, p, j * rows : (j + 1) * rows, :] = turned[g * rows : (g + 1) * rows, :]
+                if l < layers - 1:
+                    low_ref[0, c], low_ref[1, c] = gate, up
+                    if c == 0:
+                        wait(l, 2)
+                    term = dot(act.astype(BF16), wd_ref[l, cut, :])
+                    out = term if out is None else out + term
+                else:
+                    parts.append((gate, up))
+            if l < layers - 1:
+                h = (wide + out.astype(BF16).astype(F32)).astype(BF16)
+                h_ref[...] = h
+        dh = dy_ref[...]
+        right_ref[0] = dh
+        wait(layers - 1, 2)
+        for c, (gate, up) in enumerate(parts):
+            dact = dot_nt(dh, wd_ref[layers - 1, c * d : (c + 1) * d, :]).astype(BF16).astype(F32)
+            right_ref[1 + c], right_ref[1 + per + c] = silu_back(gate, up, dact)
+
+    step = pl.program_id(0)
+    pl.when(step == 0)(lambda: body(True))
+    pl.when(step > 0)(lambda: body(False))
 
 
 def chain(x, dy, wg, wu, wd, blocks, tile):
     layers, d, ff = wg.shape
     tokens = x.shape[0]
     per = ff // d
-    whole = pl.BlockSpec(memory_space=pltpu.VMEM)
     tokens_by = pl.BlockSpec((tile, d), lambda t: (t, 0))
     return pl.pallas_call(
         functools.partial(chain_kernel, layers, blocks),
         grid=(tokens // tile,),
-        in_specs=[tokens_by, tokens_by, whole, whole, whole],
+        in_specs=[tokens_by, tokens_by, *[pl.BlockSpec(memory_space=pl.ANY)] * 3],
         out_specs=[
             pl.BlockSpec((layers, per + 1, d, tile), lambda t: (0, 0, 0, t)),
             pl.BlockSpec((2 * per + 1, tile, d), lambda t: (0, t, 0)),
@@ -86,12 +110,13 @@
             jax.ShapeDtypeStruct((2, per, tokens, d), F32),
             jax.ShapeDtypeStruct((tokens, d), BF16),
         ],
+        scratch_shapes=[*(pltpu.VMEM(w.shape, BF16) for w in (wg, wu, wd)), pltpu.SemaphoreType.DMA((layers, 3))],
         compiler_params=pltpu.CompilerParams(vmem_limit_bytes=VMEM_LIMIT, dimension_semantics=("arbitrary",)),
         name="chain",
     )(x, dy, wg, wu, wd)
 
 
-def exchange_kernel(n, layers, per, wide, slots, tile, early, *refs):
+def exchange_kernel(n, layers, per, wide, slots, tile, *refs):
     (left_hbm, top_hbm, low_hbm, h_hbm, wd_hbm, wg_hbm, wu_hbm, *rest) = refs
     m_hbm, v_hbm, new_hbm, g_out, right_hbm = rest[0:3], rest[3:6], rest[6], rest[7], rest[8]
     (lbuf, rbuf, own, pair, got, state, w_new, w_tile, t_tile, g_tile, s_tile, load_sem, state_sem, pair_send, pair_recv,
@@ -199,53 +224,52 @@
     def low_result(e):
         return pltpu.make_async_copy(t_tile, right_hbm.at[1:, tokens_of(e), :], out_sem.at[1])
 
-    def extra(e):
-        @pl.when((e >= 0) & (e < tiles))
-        def _():
-            @pl.when(e == 0)
-            def _():
-                for copy in top_weights():
-                    copy.wait()
-
-            @pl.when(e > 0)
-            def _():
-                top_result(e - 1).wait()
-
-            for copy in top_inputs(e):
+    def top_step(e):
+        @pl.when(e == 0)
+        def _():
+            for copy in top_weights():
                 copy.wait()
-            da = dot_nt(t_tile[0], w_tile[0])
-            for c in range(1, 2 * per):
-                da = da + dot_nt(t_tile[c], w_tile[c])
-            da = da.astype(BF16).astype(F32)
-            wide = s_tile[1].astype(F32)
-            scale = lax.rsqrt(jnp.mean(wide * wide, -1, keepdims=True) + 1e-6)
-            mean = jnp.mean(wide * da, -1, keepdims=True)
-            dwide = da * scale - wide * (scale * scale * scale * mean)
-            s_tile[2] = (s_tile[0].astype(F32) + dwide.astype(BF16).astype(F32)).astype(BF16)
-            top_result(e).start()
-
-            @pl.when(e < tiles - 1)
-            def _():
-                for copy in top_inputs(e + 1):
-                    copy.start()
-
-            @pl.when(e == tiles - 1)
-            def _():
-                for copy in (*low_weights(), *low_inputs(e + 1)):
-                    copy.start()
-
-        @pl.when((e >= tiles) & (e < 2 * tiles))
-        def _():
-            @pl.when(e == tiles)
-            def _():
-                top_result(e - 1).wait()
-                for copy in low_weights():
-                    copy.wait()
-
-            @pl.when(e > tiles)
-            def _():
-                low_result(e - 1).wait()
-
+
+        @pl.when(e > 0)
+        def _():
+            top_result(e - 1).wait()
+
+        for copy in top_inputs(e):
+            copy.wait()
+        da = dot_nt(t_tile[0], w_tile[0])
+        for c in range(1, 2 * per):
+            da = da + dot_nt(t_tile[c], w_tile[c])
+        da = da.astype(BF16).astype(F32)
+        wide = s_tile[1].astype(F32)
+        scale = lax.rsqrt(jnp.mean(wide * wide, -1, keepdims=True) + 1e-6)
+        mean = jnp.mean(wide * da, -1, keepdims=True)
+        dwide = da * scale - wide * (scale * scale * scale * mean)
+        s_tile[2] = (s_tile[0].astype(F32) + dwide.astype(BF16).astype(F32)).astype(BF16)
+        top_result(e).start()
+
+        @pl.when(e < tiles - 1)
+        def _():
+            for copy in top_inputs(e + 1):
+                copy.start()
+
+        @pl.when(e == tiles - 1)
+        def _():
+            for copy in (*low_weights(), *low_inputs(0)):
+                copy.start()
+
+    def low_step(e):
+        @pl.when(e == 0)
+        def _():
+            top_result(tiles - 1).wait()
+            for copy in low_weights():
+                copy.wait()
+
+        @pl.when(e > 0)
+        def _():
+            low_result(e - 1).wait()
+
+        @pl.when(e < tiles)
+        def _():
             for copy in low_inputs(e):
                 copy.wait()
             for c in range(per):
@@ -253,18 +277,20 @@
                 t_tile[c], t_tile[per + c] = silu_back(g_tile[0, c], g_tile[1, c], dact)
             low_result(e).start()
 
-            @pl.when(e < 2 * tiles - 1)
-            def _():
-                for copy in low_inputs(e + 1):
-                    copy.start()
-
-        @pl.when(e == 2 * tiles)
-        def _():
-            low_result(e - 1).wait()
+        @pl.when(e < tiles - 1)
+        def _():
+            for copy in low_inputs(e + 1):
+                copy.start()
+
+    def lower(t, place):
+        turn = per_layer - 1
+        if place != 1:
+            e = 2 * (t - (turn - tiles // 2)) + place // 2
+            pl.when((e >= 0) & (e < tiles))(lambda: top_step(e))
+        e_low = 3 * (t - turn) + place
+        pl.when((e_low >= 0) & (e_low <= tiles))(lambda: low_step(e_low))
 
     start_loads(0)
-    for copy in (*top_weights(), *top_inputs(0)):
-        copy.start()
     barrier = pltpu.get_barrier_semaphore()
     for device in (fore, back, mate):
         pl.semaphore_signal(barrier, inc=1, device_id=device, device_id_type=pl.DeviceIdType.MESH)
@@ -397,9 +423,13 @@
     stages += [functools.partial(onward, s) for s in range(1, far)]
     stages += [update]
     stages += [functools.partial(gather, s) for s in range(1, far + 1)]
-    stages += [drain]
 
     def tick(t, _):
+        @pl.when(t == 1)
+        def _():
+            for copy in (*top_weights(), *top_inputs(0)):
+                copy.start()
+
         for offset in reversed(range(len(stages))):
             i = t - offset
 
@@ -408,11 +438,15 @@
                 stage(i)
 
             if offset == far + 1:
-                extra(2 * (t - early))
-        extra(2 * (t - early) + 1)
+                lower(t, 0)
+            if offset == 1:
+                lower(t, 1)
+        lower(t, 2)
+        i = t - len(stages)
+        pl.when((i >= 0) & (i < chunks))(lambda: drain(i))
         return 0
 
-    lax.fori_loop(0, chunks + len(stages) - 1, tick, 0)
+    lax.fori_loop(0, chunks + len(stages), tick, 0)
 
 
 def exchange(left, top, low, h, weights, m, v, n):
@@ -428,7 +462,7 @@
     sems = lambda *shape: pltpu.SemaphoreType.DMA(shape)
     slots = chips // 2 + 2
     return pl.pallas_call(
-        functools.partial(exchange_kernel, n, layers, per, wide, slots, tile, 3),
+        functools.partial(exchange_kernel, n, layers, per, wide, slots, tile),
         in_specs=[anywhere] * 13,
         out_specs=[anywhere, vmem, anywhere],
         out_shape=[
@@ -481,16 +515,18 @@
 def unpack(new, g, m, v, shape, n):
     layers, d, ff = shape
     per, rows = ff // d, d // n
+    halves = 1
     number = lambda l, c, kind: (layers - 1 - l) * 3 * per + kind * per + c
-    chunk = lambda kind: pl.BlockSpec((1, n, rows, d), lambda l, c: (number(l, c, kind), 0, 0, 0))
-    sums = lambda kind: pl.BlockSpec((1, rows, d), lambda l, c: (number(l, c, kind), 0, 0))
-    wide = lambda height: pl.BlockSpec((1, height, d), lambda l, c: (l, 0, c))
-    moments = [pl.BlockSpec((1, rows, d), lambda l, c: (l, c, 0)), wide(rows), wide(rows)] * 2
+    chunk = lambda kind: pl.BlockSpec((1, n // halves, rows, d), lambda l, c, k: (number(l, c, kind), k, 0, 0))
+    sums = lambda kind: pl.BlockSpec((1, rows, d), lambda l, c, k: (number(l, c, kind), 0, 0))
+    wide = pl.BlockSpec((1, d // halves, d), lambda l, c, k: (l, k, c))
+    own = pl.BlockSpec((1, rows, d), lambda l, c, k: (l, 0, c))
+    moments = [pl.BlockSpec((1, rows, d), lambda l, c, k: (l, c, 0)), own, own] * 2
     down, *rest = pl.pallas_call(
         unpack_kernel,
-        grid=(layers, per),
+        grid=(layers, per, halves),
         in_specs=[*(chunk(kind) for kind in range(3)), *(sums(kind) for kind in range(3)), *moments],
-        out_specs=[pl.BlockSpec((1, n, 1, rows, d), lambda l, c: (l, 0, c, 0, 0)), wide(d), wide(d), *moments],
+        out_specs=[pl.BlockSpec((1, n // halves, 1, rows, d), lambda l, c, k: (l, k, c, 0, 0)), wide, wide, *moments],
         out_shape=[
             jax.ShapeDtypeStruct((layers, n, per, rows, d), BF16),
             *[jax.ShapeDtypeStruct((layers, d, ff), BF16)] * 2,

time: 333 us -> 325 us (0.976)
  Pallas kernels: 332 us -> 324 us
    pallas_call x1, Pallas kernels: 67.3 us -> 61.9 us  [chain(): pl.pallas_call(functools.partial(chain_kernel, layers, blocks), grid=(tok...]
where the time goes in v3:
time: 325 us
  Pallas kernels  324 us (100%)
    pallas_call x1, Pallas kernels, exchange(): pl.pallas_call(functools.partial(exchange_kernel, n, layers, per, wide, s...  245 us
    pallas_call x1, Pallas kernels, chain(): pl.pallas_call(functools.partial(chain_kernel, layers, blocks), grid=(tok...  61.9 us
    pallas_call x1, Pallas kernels, unpack(): pl.pallas_call(unpack_kernel, grid=(layers, per, halves), in_specs=[*(chu...  17.9 us

profile of v3, /device:TPU:21, one launch (start us, length us, event | category | flops | bytes accessed | tf_op | source)
XLA Modules:
  0.0 325.3 jit_solution(16536576024107733013)
XLA Ops:
  0.6 61.9 %chain.1 = (bf16[2,4,768,2048]{3,2,1,0:T(8,128)(2,1)}, bf16[7,2048,768]{2,1,0:T(8,128)(2,1)}, f32[2,3,2048,768]{3,2,1,0:T(8,128)}, bf16[2048,768]{1,0:T(8,128)(2,1)}) custom-call(bf16[2048,768]{1,0:T(8,128)(2,1)} %bitcast.3, bf16[2048,768]{1,0:T(8,128)(2,1)} %bitcast.4, bf16[2,768,2304]{2,1,0:T(8,128)(2,1)} %refs_5_.1, bf16[2,768,2304]{2,1,0:T(8,128)(2,1)} %refs_6_.2, ...), custom_call_target="tpu_custom_call" | custom-call | tf_op jit(solution)/shard_map/chain/pallas_call | solution.py:97
  62.6 244.7 %exchange.1 = (bf16[18,16,48,768]{3,2,1,0:T(8,128)(2,1)}, bf16[18,48,768]{2,1,0:T(8,128)(2,1)}, bf16[7,2048,768]{2,1,0:T(8,128)(2,1)}) custom-call(bf16[2,4,768,2048]{3,2,1,0:T(8,128)(2,1)} %get-tuple-element.24.refs_0_, bf16[7,2048,768]{2,1,0:T(8,128)(2,1)} %get-tuple-element.25.refs_1_, f32[2,3,2048,768]{3,2,1,0:T(8,128)} %get-tuple-element.26.refs_2_, ...), custom_call_target="tpu_custom_call" | custom-call | tf_op jit(solution)/shard_map/exchange/pallas_call | solution.py:464
  307.3 17.9 %unpack.1 = (bf16[2,16,3,48,768]{4,3,2,1,0:T(8,128)(2,1)}, bf16[2,768,2304]{2,1,0:T(8,128)(2,1)}, bf16[2,768,2304]{2,1,0:T(8,128)(2,1)}, f32[2,144,768]{2,1,0:T(...) custom-call(bf16[18,16,48,768]{3,2,1,0:T(8,128)(2,1)} %get-tuple-ele, ...), custom_call_target="tpu_custom_call" | custom-call | tf_op jit(solution)/shard_map/unpack/pallas_call | solution.py:525
